TPU v7x, 256 devices: a whole 4x4x8 slice. The times are simulated.
256 devices in a mesh: rep: 2 (over core), dp: 128 (over x, y, z).
Axes of the slice: x: 4, y: 4, z: 8, core: 2. Of those that a mesh axis runs over, the one named last changes fastest.
Arguments:
- g_w_gate: bfloat16 [256, 2, 896, 2560], P(('rep', 'dp')), parts along dimension 0
- g_w_up: bfloat16 [256, 2, 896, 2560], P(('rep', 'dp')), parts along dimension 0
- g_w_down: bfloat16 [256, 2, 2560, 896], P(('rep', 'dp')), parts along dimension 0
- w_gate: bfloat16 [2, 896, 2560], replicated
- w_up: bfloat16 [2, 896, 2560], replicated
- w_down: bfloat16 [2, 2560, 896], replicated
- m_w_gate: float32 [2, 896, 2560], P(None, 'dp')
- m_w_up: float32 [2, 896, 2560], P(None, 'dp')
- m_w_down: float32 [2, 2560, 896], P(None, 'dp')
- v_w_gate: float32 [2, 896, 2560], P(None, 'dp')
- v_w_up: float32 [2, 896, 2560], P(None, 'dp')
- v_w_down: float32 [2, 2560, 896], P(None, 'dp')
Outputs:
- output 1: bfloat16 [4, 896, 2560], P('rep'), parts along dimension 0
- output 2: bfloat16 [4, 896, 2560], P('rep'), parts along dimension 0
- output 3: bfloat16 [4, 2560, 896], P('rep'), parts along dimension 0
- output 4: float32 [4, 896, 2560], P('rep', 'dp'), parts along dimension 0
- output 5: float32 [4, 896, 2560], P('rep', 'dp'), parts along dimension 0
- output 6: float32 [4, 2560, 896], P('rep', 'dp'), parts along dimension 0
- output 7: float32 [4, 896, 2560], P('rep', 'dp'), parts along dimension 0
- output 8: float32 [4, 896, 2560], P('rep', 'dp'), parts along dimension 0
- output 9: float32 [4, 2560, 896], P('rep', 'dp'), parts along dimension 0
There are 2 independent parts. A program takes and returns all parts, laid end to end along the dimension named above; an argument that names none is the same for every part.
All inputs are finite; a program needn't handle non-finite values.
Results may differ from a plain program's by a relative error of at most 0.022.
Values are sent between devices in bfloat16 or wider.
A program may use at most 768 MiB of HBM per device.

v0:
```python
import jax
import jax.numpy as jnp
from jax import lax
from jax.sharding import PartitionSpec as P


def adamw(w, m, v, g):
    m = 0.9 * m + 0.1 * g
    v = 0.95 * v + 0.05 * g * g
    step = m * lax.rsqrt(v + 1e-8) + 0.1 * w
    return (w - 0.02 * step).astype(jnp.bfloat16), m, v


def clipped(gradients, sum_of_squares, count):
    factor = jnp.minimum(1.0, 0.5 * lax.rsqrt(sum_of_squares / count + 1e-30))
    return [g * factor for g in gradients]


def solution(mesh):
    def step(*arrays):
        terms, weights, m, v = (arrays[i : i + 3] for i in (0, 3, 6, 9))
        gradients = [lax.psum_scatter(t[0], "dp", scatter_dimension=1, tiled=True).astype(jnp.float32) for t in terms]
        squares = lax.psum(sum(jnp.sum(g * g) for g in gradients), "dp")
        gradients = clipped(gradients, squares, lax.psum(1, "dp") * sum(g.size for g in gradients))
        me = lax.axis_index("dp")
        own = [lax.dynamic_slice_in_dim(w, me * one.shape[1], one.shape[1], 1).astype(jnp.float32) for w, one in zip(weights, m, strict=True)]
        new = [adamw(w, m, v, g) for w, m, v, g in zip(own, m, v, gradients, strict=True)]
        whole = [lax.all_gather(one[0], "dp", axis=1, tiled=True) for one in new]
        return (*whole, *(one[1] for one in new), *(one[2] for one in new))

    all_of, cut = P(None, None, None), P(None, "dp", None)
    return jax.shard_map(
        step,
        mesh=mesh,
        in_specs=(P(("rep", "dp"), None, None, None),) * 3 + (all_of,) * 3 + (cut,) * 6,
        out_specs=(P("rep", None, None),) * 3 + (P("rep", "dp", None),) * 6,
        check_vma=False,
    )
```

profile of v0, /device:TPU:2, one launch (start us, length us, event | category | flops | bytes accessed | tf_op | source)
XLA Modules:
  0.0 1297.2 jit_solution(7209120091978421236)
XLA Ops:
  7.2 0.0 all-reduce.6.cloned.1.call-start
  7.2 0.0 copy-start
  7.2 0.0 slice-start
  7.2 0.0 slice-start.1
  7.3 41.0 %copy.48 = bf16[1,2,2560,896]{3,1,2,0:T(2,128)(2,1)} copy(bf16[1,2,2560,896]{3,2,1,0:T(8,128)(2,1)} %param.14) | data formatting | bytes 18350080 | tf_op args[2]
  48.2 0.0 copy-done
  48.2 0.0 slice-start.2
  48.2 26.1 %copy.49 = bf16[1,2,896,2560]{3,1,2,0:T(2,128)(2,1)} copy(bf16[1,2,896,2560]{3,2,1,0:T(8,128)(2,1)S(1)} %copy-done) | data formatting | bytes 18350080 | tf_op args[1]
  74.4 0.0 slice-done
  74.4 0.0 slice-done.1
  74.4 0.0 slice-done.2
  74.4 26.1 %copy.50 = bf16[1,2,896,2560]{3,1,2,0:T(2,128)(2,1)} copy(bf16[1,2,896,2560]{3,2,1,0:T(8,128)(2,1)S(1)} %bitcast.14) | data formatting | bytes 18350080 | tf_op args[0]
  100.5 0.0 copy-start.7
  100.5 0.0 copy-start.1
  100.5 0.0 copy-start.3
  100.5 0.0 copy-start.4
  100.5 0.0 copy-start.5
  100.6 0.0 copy-start.6
  100.6 0.0 all-reduce.6.cloned.1.call-update
  100.6 0.0 all-gather.6.cloned.1.call-start
  100.6 0.5 copy-done.7
  101.2 0.6 dynamic-slice
  103.1 451.6 %all-reduce.6.cloned.1.call-done = (bf16[2,896,2560]{2,0,1:T(2,128)(2,1)}, bf16[2,896,2560]{2,0,1:T(2,128)(2,1)}, bf16[2,2560,896]{2,0,1:T(2,128)(2,1)}) async-done(((bf16[2,896,2560]{2,0,1:T(2,128)(2,1)}, bf16[2,896,2560]{2,0,1:T(2,128)(2,1)}, bf16[2,2560,896]{2,0,1:T(2,128)(2,1)}), (bf16[2,896,2560]{2,0,1:T(2,128)(2,1)}, bf16[2,896,2560]{2,0,1:T(2,128)(2,1)}, ...) | async-done | bytes 27525136
  554.7 1.7 fusion.8
  557.7 1.6 fusion.10
  559.9 1.1 constant_dynamic-slice_fusion.1
  561.0 307.6 %psum.7 = f32[]{:T(128)} all-reduce(f32[]{:T(128)S(6)} %add.65), channel_id=1, replica_groups=mesh['rep'=2,'dp'=128] {'dp'}, use_global_device_ids=true, to_apply=%region_6.0 | all-reduce | flops 1 | bytes 8 | tf_op jit(solution)/shard_map/psum | solution.py:23
  869.3 0.0 copy-done.1
  869.4 0.0 copy-done.2
  869.4 2.0 fusion.19
  871.3 0.0 all-gather.6.cloned.1.call-update
  871.4 0.0 all-gather.4.cloned.1.call-start
  871.4 0.0 copy-done.3
  871.4 0.0 copy-done.4
  871.4 2.0 fusion.18
  873.4 0.0 all-gather.4.cloned.1.call-update
  873.4 0.2 all-gather.8.cloned.1.call-start
  873.7 0.9 constant_dynamic-slice_fusion
  874.6 0.0 copy-done.5
  874.6 0.0 copy-done.6
  874.6 2.0 fusion.20
  876.6 0.0 all-gather.8.cloned.1.call-update
  876.7 152.2 %all-gather.6.cloned.1.call-done = bf16[2,896,2560]{2,0,1:T(2,128)(2,1)} async-done(((bf16[2,7,2560]{2,0,1:T(2,128)(2,1)}), bf16[2,896,2560]{2,0,1:T(2,128)(2,1)}) %all-gather.6.cloned.1.call-update) | async-done | bytes 9175056 | tf_op jit(solution)/shard_map/all_gather | solution.py:28
  1028.9 8.7 copy.37
  1037.6 118.4 %all-gather.4.cloned.1.call-done = bf16[2,896,2560]{2,0,1:T(2,128)(2,1)} async-done(((bf16[2,7,2560]{2,0,1:T(2,128)(2,1)}), bf16[2,896,2560]{2,0,1:T(2,128)(2,1)}) %all-gather.4.cloned.1.call-update) | async-done | bytes 9175056 | tf_op jit(solution)/shard_map/all_gather | solution.py:28
  1155.9 8.7 copy.36
  1164.6 117.6 %all-gather.8.cloned.1.call-done = bf16[2,2560,896]{2,0,1:T(2,128)(2,1)} async-done(((bf16[2,20,896]{2,0,1:T(2,128)(2,1)}), bf16[2,2560,896]{2,0,1:T(2,128)(2,1)}) %all-gather.8.cloned.1.call-update) | async-done | bytes 9175056 | tf_op jit(solution)/shard_map/all_gather | solution.py:28
  1282.2 8.4 copy.38
  (2 shorter events, 0.0 us)
Async XLA Ops:
  7.2 547.5 %all-reduce.6.cloned.1.call-start = ((), (), s32[]{:S(2)}) async-start(), calls=%async_computation.3 | async-start | bytes 55050240
  7.2 41.0 %copy-start = (bf16[1,2,896,2560]{3,2,1,0:T(8,128)(2,1)S(1)}, bf16[1,2,896,2560]{3,2,1,0:T(8,128)(2,1)}, u32[]{:S(2)}) copy-start(bf16[1,2,896,2560]{3,2,1,0:T(8,128)(2,1)} %param.13) | copy-start | bytes 27525124
  7.2 67.1 %slice-start = ((s8[9175040]{0:T(1024)(128)(4,1)}), s8[4194304]{0:T(1024)(128)(4,1)S(1)}, s32[]{:S(2)}) async-start(s8[9175040]{0:T(1024)(128)(4,1)} %bitcast.13), calls=%async_computation.4 | async-start | bytes 8388608
  7.2 67.1 %slice-start.1 = ((s8[9175040]{0:T(1024)(128)(4,1)}), s8[4194304]{0:T(1024)(128)(4,1)S(1)}, s32[]{:S(2)}) async-start(s8[9175040]{0:T(1024)(128)(4,1)} %bitcast.13), calls=%async_computation.5 | async-start | bytes 8388608
  48.2 26.1 %slice-start.2 = ((s8[9175040]{0:T(1024)(128)(4,1)}), s8[786432]{0:T(1024)(128)(4,1)S(1)}, s32[]{:S(2)}) async-start(s8[9175040]{0:T(1024)(128)(4,1)} %bitcast.13), calls=%async_computation.6 | async-start | bytes 1572864
  100.5 0.7 copy-start.7
  100.5 768.8 %copy-start.1 = (f32[2,7,2560]{2,0,1:T(2,128)S(1)}, f32[2,7,2560]{2,0,1:T(2,128)}, u32[]{:S(2)}) copy-start(f32[2,7,2560]{2,0,1:T(2,128)} %param.22) | copy-start | bytes 430084
  100.5 768.8 %copy-start.2 = (f32[2,7,2560]{2,0,1:T(2,128)S(1)}, f32[2,7,2560]{2,0,1:T(2,128)}, u32[]{:S(2)}) copy-start(f32[2,7,2560]{2,0,1:T(2,128)} %param.19) | copy-start | bytes 430084
  100.5 770.9 %copy-start.3 = (f32[2,7,2560]{2,0,1:T(2,128)S(1)}, f32[2,7,2560]{2,0,1:T(2,128)}, u32[]{:S(2)}) copy-start(f32[2,7,2560]{2,0,1:T(2,128)} %param.21) | copy-start | bytes 430084
  100.5 770.9 %copy-start.4 = (f32[2,7,2560]{2,0,1:T(2,128)S(1)}, f32[2,7,2560]{2,0,1:T(2,128)}, u32[]{:S(2)}) copy-start(f32[2,7,2560]{2,0,1:T(2,128)} %param.18) | copy-start | bytes 430084
  100.5 774.1 %copy-start.5 = (f32[2,20,896]{2,0,1:T(2,128)S(1)}, f32[2,20,896]{2,0,1:T(2,128)}, u32[]{:S(2)}) copy-start(f32[2,20,896]{2,0,1:T(2,128)} %param.23) | copy-start | bytes 430084
  100.6 774.1 %copy-start.6 = (f32[2,20,896]{2,0,1:T(2,128)S(1)}, f32[2,20,896]{2,0,1:T(2,128)}, u32[]{:S(2)}) copy-start(f32[2,20,896]{2,0,1:T(2,128)} %param.20) | copy-start | bytes 430084
  100.6 928.3 %all-gather.6.cloned.1.call-start = ((), (), s32[]{:S(2)}) async-start(), calls=%async_computation.1 | async-start | bytes 9246720 | tf_op jit(solution)/shard_map/all_gather | solution.py:28
  871.4 284.6 %all-gather.4.cloned.1.call-start = ((), (), s32[]{:S(2)}) async-start(), calls=%async_computation | async-start | bytes 9246720 | tf_op jit(solution)/shard_map/all_gather | solution.py:28
  873.4 408.8 %all-gather.8.cloned.1.call-start = ((), (), s32[]{:S(2)}) async-start(), calls=%async_computation.2 | async-start | bytes 9246720 | tf_op jit(solution)/shard_map/all_gather | solution.py:28
Sparse Core Ops, SparseCore 0:
  100.7 453.9 all-reduce.5
  871.5 157.3 all-gather.5
  1033.2 122.7 all-gather.3
  1159.5 122.7 all-gather.7
where the time goes:
time: 1300 us
  waiting for transfers between devices  840 us (65%)
  blocking collectives  308 us (24%)
  local copies, waits for them, and re-layouts  122 us (9%)
  between operations  17.9 us (1%)
    unnamed x5, waiting for transfers between devices  452 us
    all_gather x3, waiting for transfers between devices, step(): whole = [lax.all_gather(one[0], 'dp', axis=1, tiled=True) for one in new]  388 us
    psum x1, blocking collectives, step(): squares = lax.psum(sum((jnp.sum(g * g) for g in gradients)), 'dp')  308 us
    unnamed x29, local copies, waits for them, and re-layouts  120 us
  transfers between devices with their start and end apart: 4, of which 4 were waited for; matrix products, arithmetic and copies ran while one was open for 2% of the time, Pallas kernels for 0%

commit v1 on v0

v1 whole, which is shorter than its diff:
```python
import jax
import jax.numpy as jnp
from jax import lax
from jax.experimental import pallas as pl
from jax.experimental.pallas import tpu as pltpu
from jax.sharding import PartitionSpec as P

MESH = pl.DeviceIdType.MESH
F32, BF16 = jnp.float32, jnp.bfloat16
X, Y, Z = 4, 4, 8
SIZE = {"x": X, "y": Y, "z": Z}
DIMS = {"A": ("x", "y", "z"), "B": ("y", "z", "x"), "C": ("z", "x", "y")}
COLOURS = tuple(DIMS)
LAYERS, ROWS, LANES = 2, 8, 128
TILE = (ROWS, LANES)
D, FF = 896, 2560
HIGH, HALF, LEFT, PART = 7, 10, 6, 5
BLOCK = {"A": (HIGH, LEFT), "B": (PART, HIGH), "C": (HIGH, HALF - LEFT)}
COUNT = 3 * LAYERS * D * FF


def lens(c):
    return tuple(SIZE[d] for d in DIMS[c])


def tiles(c):
    return BLOCK[c][0] * BLOCK[c][1]


def down_place(z):
    return (0, (z + 1) // 2 % X) if z % 2 else (1, (z // 2 + 3) % X)


def ring(n, ant):
    return [(ant, n // 2)] + [(d, k) for k in range(n // 2 - 1, 0, -1) for d in (1, -1)]


def slots(n, ant):
    return {m: i for i, m in enumerate(sorted(ring(n, ant), key=lambda m: (m[1], -m[0])))}


def far_first(n):
    return [n // 2] + [s * k for k in range(n // 2 - 1, 0, -1) for s in (1, -1)] + [0]


def ant_of(o):
    return -1 if o % 2 else 1


def ant_in(phase, unit):
    return (1, ant_of(sum(o for o in unit if o is not None)) if unit else 1)[phase < 3]


def came(c, phase, unit, n, o):
    far = n - o < n // 2 or (n == 2 * o and ant_in(phase, unit) == 1)
    return (c, phase, unit, 1, n - o) if far else (c, phase, unit, -1, o)


def gather_messages():
    out = {}
    for c in COLOURS:
        n1, n2, n3 = lens(c)

        def add(phase, unit, count, first):
            dim = DIMS[c][phase - 1]
            for d, k in ring(SIZE[dim], ant_in(phase, unit)):
                out[c, phase, unit, d, k] = ((dim, d), count * tiles(c), [(c, phase, unit, d, k - 1)] if k > 1 else first)

        add(3, (), 1, [])
        for o in range(n3):
            first = [came(c, 3, (), n3, o)] if o else []
            add(2, (o,), 1, first)
            add(1, (0, o), 1, first)
        for o in range(1, n2):
            add(1, (o, None), n3, [came(c, 2, (i,), n2, o) for i in range(n3)])
    return out


def ordered(messages, slack, latency, rate):
    users, tail = {t: [] for t in messages}, {}
    for t, (_, _, waits) in messages.items():
        for w in waits:
            users[w].append(t)

    def way(t):
        if t not in tail:
            tail[t] = 2 * messages[t][1] / rate + latency + max((way(u) for u in users[t]), default=0)
        return tail[t]

    for t in messages:
        way(t)
    queues = {m[0]: [] for m in messages.values()}
    left, arrives, now, starts = list(messages), {}, 0.0, []
    while left or any(queues.values()):
        ready = [
            t
            for t in left
            if all(arrives.get(w, now + 1) <= now for w in messages[t][2]) and 2 * sum(q[1] for q in queues[messages[t][0]]) <= slack
        ]
        if ready:
            t = max(ready, key=way)
            left.remove(t)
            starts.append(t)
            queues[messages[t][0]].append([t, messages[t][1] / rate])
            continue
        speed = {(m, d): 1 / 2 if queues[m, -d] else 1 for (m, d), q in queues.items() if q}
        full = {link: sum(q[1] for q in queues[link]) - slack / 2 for link in speed}
        events = [queues[link][0][1] / s for link, s in speed.items()] + [full[link] / s for link, s in speed.items() if full[link] > 0]
        pause = min(events + [a - now for a in arrives.values() if a > now]) + 1e-6
        now += pause
        for link, s in speed.items():
            queues[link][0][1] -= pause * s
            if queues[link][0][1] <= 0:
                arrives[queues[link].pop(0)[0]] = now + latency
    return starts, list(arrives), arrives


GATHER = gather_messages()
GATHER_ORDER, ENDS, GATHER_AT = ordered(GATHER, 2.0, 2.0, 43.0)


def back(t):
    c, phase, unit, d, k = t
    return (c, phase, unit, -d, k)


REDUCE = {back(t): (link, n, []) for t, (link, n, _) in GATHER.items()}
for t, (_, _, waits) in GATHER.items():
    for w in waits:
        REDUCE[back(w)][2].append(back(t))
REDUCE_ORDER = [back(t) for t in reversed(ENDS)]
R_ID = {t: i for i, t in enumerate(REDUCE)}
G_ID = {t: i for i, t in enumerate(GATHER)}


class Place:
    def __init__(self):
        dp = lax.axis_index("dp")
        rep = lax.axis_index("rep")
        self.at = at = {"x": lax.div(dp, Y * Z), "y": lax.rem(lax.div(dp, Z), Y), "z": lax.rem(dp, Z)}
        sign = 1 - 2 * rep
        self.offset = {(d, k): lax.rem(at[d] + sign * k + n, n) for d, n in SIZE.items() for k in range(-n // 2, n // 2) if k}

        def device(**moved):
            a = {**at, **moved}
            return (rep, (a["x"] * Y + a["y"]) * Z + a["z"])

        def ahead(d, k):
            return lax.rem(at[d] + SIZE[d] + k, SIZE[d])

        self.device = device
        self.beside = {(d, e): device(**{d: self.offset[d, e]}) for d in SIZE for e in (1, -1)}
        self.line = [ahead("z", k) for k in range(Z)]
        self.line_from = [ahead("z", -k) for k in range(Z)]
        self.line_device = [device(z=to) for to in self.line]
        self.plane_device = [device(x=ahead("x", k // Y), y=ahead("y", k % Y)) for k in range(X * Y)]
        self.plane_from = [Y * ahead("x", -(k // Y)) + ahead("y", -(k % Y)) for k in range(X * Y)]

    def off(self, dim, k):
        n = SIZE[dim]
        k = (k + n // 2) % n - n // 2
        return self.offset[dim, k] if k else self.at[dim]


def fence(p):
    peers = p.line_device[1:] + p.plane_device[1:]
    barrier = pltpu.get_barrier_semaphore()
    for peer in peers:
        pl.semaphore_signal(barrier, inc=1, device_id=peer, device_id_type=MESH)
    pl.semaphore_wait(barrier, len(peers))


def start_loads(p, gate, up, down, T, sem):
    for step in range(Z):
        for c in COLOURS:
            n1 = lens(c)[0]
            if step >= n1:
                continue
            k = far_first(n1)[step]
            j = p.off(DIMS[c][0], k)
            s = sem[c].at[k % n1]
            if c == "A":
                for z in range(Z):
                    src = (gate, up)[z // X].at[z // 2 % 2, j, :, :, z % 2, pl.ds(0, LEFT)]
                    pltpu.make_async_copy(src, T[c].at[j, :, z], s).start()
            elif c == "B":
                for z in range(Z):
                    layer, q = down_place(z)
                    pltpu.make_async_copy(down.at[layer, :, j, q], T[c].at[j, z], s).start()
            else:
                layer, half = lax.rem(lax.div(j, 2), 2), lax.rem(j, 2)

                def load(ref):
                    pltpu.make_async_copy(ref.at[layer, :, :, :, half, pl.ds(LEFT, HALF - LEFT)], T[c].at[j], s).start()

                pl.when(j < X)(lambda: load(gate))
                pl.when(j >= X)(lambda: load(up))


class Reduce:
    def __init__(self, p, T, O, load, sent, arrived):
        self.p, self.T, self.O, self.load, self.sent, self.arrived = p, T, O, load, sent, arrived
        self.waited, self.loaded = set(), set()

    def areas(self, t):
        c, phase, unit, d, k = t
        n1, n2, n3 = lens(c)
        d1, d2, d3 = DIMS[c]
        p = self.p
        slot = slots(SIZE[DIMS[c][phase - 1]], -ant_in(phase, unit))[d, k]
        if phase == 1:
            j2 = p.off(d2, unit[0])
            first, count = (0, n3) if unit[1] is None else (p.off(d3, unit[1]), 1)
            return (p.off(d1, d * k), j2), first, (slot, j2), first, count
        if phase == 2:
            j3 = p.off(d3, unit[0])
            return (p.at[d1], p.off(d2, d * k)), j3, (n1 - 1, slot), j3, 1
        return (p.at[d1], p.at[d2]), p.off(d3, d * k), (n1 - 1, n2 - 1), slot, 1

    def copy(self, t):
        c, phase, _, d, _ = t
        src, i, dst, j, n = self.areas(t)
        s = R_ID[t]
        return pltpu.make_async_remote_copy(
            src_ref=self.T[c].at[(*src, pl.ds(i, n))],
            dst_ref=self.O[c].at[(*dst, pl.ds(j, n))],
            send_sem=self.sent.at[s],
            recv_sem=self.arrived.at[s],
            device_id=self.p.beside[DIMS[c][phase - 1], d],
            device_id_type=MESH,
        )

    def wait(self, t):
        if t not in self.waited:
            self.waited.add(t)
            self.copy(t).wait_recv()

    def wait_load(self, c, k):
        k %= lens(c)[0]
        if (c, k) not in self.loaded:
            self.loaded.add((c, k))
            ref = self.T[c].at[self.p.off(DIMS[c][0], k)]
            pltpu.make_async_copy(ref, ref, self.load[c].at[k]).wait()

    def ended(self, c, phase, j2, j3):
        last = lens(c)[0] - 1
        return [(0, j2, j3), (1, j2, j3), (last, 0, j3), (last, 1, j3)][: 2 * (phase - 1)]

    def send(self, t):
        c, phase, unit, d, k = t
        T, O = self.T[c], self.O[c]
        for w in REDUCE[t][2]:
            self.wait(w)
        self.wait_load(c, d * k if phase == 1 else 0)
        src, first, _, _, count = self.areas(t)
        before = (c, phase, unit, d, k + 1)
        chain = before in R_ID
        if phase > 1 or chain:
            _, _, there, start, _ = self.areas(before if chain else t)

            def one(i):
                parts = self.ended(c, phase, src[1], first + i)
                if chain:
                    parts.append((*there, start + i))
                total = T[(*src, first + i)].astype(F32)
                for part in parts:
                    total = total + O[part].astype(F32)
                T[(*src, first + i)] = total.astype(BF16)

            if count == 1:
                one(0)
            else:
                pl.loop(0, count)(one)
        self.copy(t).start()

    def own(self, c):
        n1, n2, _ = lens(c)
        for t in REDUCE:
            if t[0] == c and t[-1] == 1 and t[2] in ((), (0,), (0, 0)):
                self.wait(t)
        self.wait_load(c, 0)
        i, j, k = (self.p.at[d] for d in DIMS[c])
        total = self.T[c][i, j, k].astype(F32)
        for part in self.ended(c, 3, j, k) + [(n1 - 1, n2 - 1, e) for e in (0, 1)]:
            total = total + self.O[c][part].astype(F32)
        return total.astype(BF16).astype(F32)


class Gather:
    def __init__(self, p, O, sent, arrived):
        self.p, self.O, self.sent, self.arrived = p, O, sent, arrived
        self.waited = set()

    def copy(self, t, came=0):
        c, phase, unit, d, k = t
        d1, d2, d3 = DIMS[c]
        p, dim = self.p, DIMS[c][phase - 1]
        behind = p.off(dim, d * (1 - came - k))
        if phase == 1:
            at = (behind, p.off(d2, unit[0])) if unit[1] is None else (behind, p.off(d2, unit[0]), p.off(d3, unit[1]))
        else:
            at = (p.at[d1], behind, p.off(d3, unit[0])) if phase == 2 else (p.at[d1], p.at[d2], behind)
        ref, s = self.O[c].at[at], G_ID[t]
        return pltpu.make_async_remote_copy(
            src_ref=ref, dst_ref=ref, send_sem=self.sent.at[s], recv_sem=self.arrived.at[s], device_id=p.beside[dim, d], device_id_type=MESH
        )

    def wait(self, t):
        if t not in self.waited:
            self.waited.add(t)
            self.copy(t, 1).wait_recv()

    def send(self, t):
        for w in GATHER[t][2]:
            self.wait(w)
        self.copy(t).start()


def rows_of(a):
    return lax.broadcasted_iota(jnp.int32, a.shape, a.ndim - 2)


def joined(a, b, k):
    return pltpu.roll(jnp.where(rows_of(b) >= ROWS - k, a, b), k, b.ndim - 2)


def adamw(w, m, v, g):
    m = 0.9 * m + 0.1 * g
    v = 0.95 * v + 0.05 * g * g
    return w - 0.02 * (m * lax.rsqrt(v + 1e-8) + 0.1 * w), m, v


DOWN_ROWS = (ROWS, ROWS, ROWS // 2)
SCRATCH = {
    "raw": ((2, 2, HIGH, LAYERS, FF), F32),
    "raw_down": ((2, 20, LAYERS, D), F32),
    "old": ((2, LAYERS, 2, 2, HALF, *TILE), BF16),
    "old_down": ((LAYERS, 3, HIGH, *TILE), BF16),
    "w": ((2, LAYERS, 2 * HALF, *TILE), F32),
    "w_low": ((LAYERS, 3, HIGH, *TILE), F32),
    "mv": ((2, 2, LAYERS, 2 * HALF, *TILE), F32),
    "mv_low": ((2, LAYERS, 3, HIGH, *TILE), F32),
    "out": ((Z, HALF, *TILE), BF16),
    "into": ((Z, HALF, *TILE), BF16),
    "out_low": ((2, 3, HIGH, *TILE), BF16),
    "into_low": ((LAYERS, 3, HIGH, *TILE), BF16),
    "new": ((Z, HALF, *TILE), BF16),
    "news": ((Z, HALF, *TILE), BF16),
    "new_low": ((LAYERS, 3, HIGH, *TILE), BF16),
    "news_low": ((2, 3, HIGH, *TILE), BF16),
    "z_sum": ((Z, *TILE), F32),
    "sum": ((X * Y, *TILE), F32),
}


class Few:
    def __init__(self, p, sent, arrived):
        self.p, self.sent, self.arrived, self.pushed, self.used = p, sent, arrived, [], 0

    def places(self, n):
        self.used += n
        return self.used - n

    def push(self, src, dst, i, j, to):
        one = pltpu.make_async_remote_copy(
            src_ref=src, dst_ref=dst, send_sem=self.sent.at[i], recv_sem=self.arrived.at[j], device_id=to, device_id_type=MESH
        )
        self.pushed.append(one)
        one.start()

    def arrive(self, ref, i):
        pltpu.make_async_copy(ref, ref, self.arrived.at[i]).wait()

    def line(self, out, into):
        p, base = self.p, self.places(Z)
        z = p.at["z"]
        for k in range(1, Z):
            self.push(out.at[p.line[k]], into.at[z], base + k, base + k, p.line_device[k])

        def wait():
            for k in range(1, Z):
                self.arrive(into.at[p.line_from[k]], base + k)

        return wait


def lanes(c):
    return pl.ds(pl.multiple_of(c * LANES, LANES), LANES)


def work(*refs):
    terms, weights, moments, refs = refs[:3], refs[3:6], refs[6:12], refs[12:]
    outs, made, refs = refs[:3], refs[3:9], refs[9:]
    O, T, refs = dict(zip(COLOURS, outs)), dict(zip(COLOURS, refs)), refs[3:]
    s = dict(zip(SCRATCH, refs))
    *load, small, r_sent, r_arrived, g_sent, g_arrived, x_sent, x_arrived = refs[len(SCRATCH) :]
    p = Place()
    x, y, z = p.at.values()
    start_loads(p, *terms, T, dict(zip(COLOURS, load)))

    plain = []

    def fetch(src, dst):
        plain.append(pltpu.make_async_copy(src, dst, small.at[len(plain)]))
        plain[-1].start()

    first = (X * Y * PART) * x + 20 * y + lax.div(PART * z, 2)
    for layer in range(LAYERS):
        for w in range(2):
            for i, row in enumerate((lax.max(z - 1, 0), lax.min(z, HIGH - 1))):
                fetch(weights[w].at[layer, x, y, row], s["old"].at[w, layer, i])
        fetch(weights[2].at[layer, pl.ds(first, 3)], s["old_down"].at[layer])
    for i in range(2):
        for w in range(2):
            fetch(moments[3 * i + w], s["raw"].at[i, w])
        fetch(moments[3 * i + 2], s["raw_down"].at[i])

    def unpack():
        for one in plain:
            one.wait()
        for layer in range(LAYERS):
            for w in range(2):
                low, high = (s["old"][w, layer, i].reshape(2 * HALF, *TILE).astype(F32) for i in range(2))
                s["w"][w, layer] = joined(low, high, z)
            part = [s["old_down"][layer, j].astype(F32) for j in range(3)]
            for j in range(3):
                s["w_low"][layer, j] = jnp.where(lax.rem(z, 2) == 1, joined(part[j], part[min(j + 1, 2)], ROWS // 2), part[j])

        @pl.loop(0, 2 * HALF)
        def _(c):
            for i in range(2):
                for w in range(2):
                    for layer in range(LAYERS):
                        s["mv"][i, w, layer, c, pl.ds(0, HIGH)] = s["raw"][i, w, :, layer, lanes(c)]

        @pl.loop(0, HIGH)
        def _(c):
            for i in range(2):
                for layer in range(LAYERS):
                    for j, n in enumerate(DOWN_ROWS):
                        s["mv_low"][i, layer, j, c, pl.ds(0, n)] = s["raw_down"][i, pl.ds(ROWS * j, n), layer, lanes(c)]

    fence(p)
    reduce = Reduce(p, T, O, dict(zip(COLOURS, load)), r_sent, r_arrived)
    for n, t in enumerate(REDUCE_ORDER):
        if 2 * n == len(REDUCE_ORDER):
            unpack()
        reduce.send(t)

    few = Few(p, x_sent, x_arrived)
    squares = jnp.zeros(TILE, F32)
    for c in ("C", "A"):
        g = reduce.own(c)
        n = BLOCK[c][1]
        place = pl.ds(0 if c == "A" else LEFT, n)
        squares = squares + jnp.sum((g * g).reshape(HIGH * n, *TILE), axis=0)
        for k in range(Z):
            before, at = g[max(k - 1, 0)], g[min(k, HIGH - 1)]
            s["out"][k, place] = (joined(before, at, k) if k else at).astype(BF16)
    pieces = few.line(s["out"], s["into"])
    s["into"][z] = s["out"][z]

    g = reduce.own("B")
    squares = squares + jnp.sum((g * g).reshape(PART * HIGH, *TILE), axis=0)
    for j in range(3):
        s["out_low"][0, j] = g[j].astype(BF16)
        s["out_low"][1, j] = joined(g[2 + j], g[min(3 + j, PART - 1)], ROWS // 2).astype(BF16)
    my_layer = 1 - lax.rem(z, 2)
    my_pair = lax.rem(lax.div(z + 1, 2) + 3 * my_layer, X)
    low = few.places(2)
    for i in range(2):
        few.push(s["out_low"].at[i], s["into_low"].at[my_layer], low + i, low + my_layer, p.device(z=2 * my_pair + i))

    base = few.places(Z)
    s["z_sum"][z] = squares
    for k in range(1, Z):
        few.push(s["z_sum"].at[z], s["z_sum"].at[z], base + k, base + k, p.line_device[k])
    for k in range(1, Z):
        few.arrive(s["z_sum"].at[p.line_from[k]], base + k)
    base, mine = few.places(X * Y), Y * x + y
    s["sum"][mine] = jnp.sum(s["z_sum"][...], axis=0)
    for k in range(1, X * Y):
        few.push(s["sum"].at[mine], s["sum"].at[mine], base + k, base + k, p.plane_device[k])
    pieces()
    for layer in range(LAYERS):
        few.arrive(s["into_low"].at[layer], low + layer)
    for k in range(1, X * Y):
        few.arrive(s["sum"].at[p.plane_from[k]], base + k)
    total = jnp.sum(s["sum"][...], axis=0)
    total = jnp.sum(jnp.sum(total, axis=1, keepdims=True), axis=0, keepdims=True)
    factor = jnp.minimum(1.0, 0.5 * lax.rsqrt(total / COUNT + 1e-30))

    for owner in range(Z):
        w, layer, part = owner // X, owner // 2 % 2, pl.ds(owner % 2 * HALF, HALF)
        g = s["into"][owner].astype(F32) * factor
        new, m, v = adamw(s["w"][w, layer, part], s["mv"][0, w, layer, part], s["mv"][1, w, layer, part], g)
        s["mv"][0, w, layer, part], s["mv"][1, w, layer, part] = m, v
        s["new"][owner] = new.astype(BF16)
    back_pieces = few.line(s["new"], s["news"])
    for layer in range(LAYERS):
        g = s["into_low"][layer].astype(F32) * factor
        new, m, v = adamw(s["w_low"][layer], s["mv_low"][0, layer], s["mv_low"][1, layer], g)
        s["mv_low"][0, layer], s["mv_low"][1, layer] = m, v
        s["new_low"][layer] = new.astype(BF16)
    s["news"][z] = s["new"][z]
    low, parity = few.places(2), lax.rem(z, 2)
    for layer in range(LAYERS):
        to = lax.rem(z - parity + (Z - 1, 2)[layer], Z)
        few.push(s["new_low"].at[layer], s["news_low"].at[parity], low + layer, low + parity, p.device(z=to))

    own = {c: tuple(p.at[d] for d in DIMS[c]) for c in COLOURS}
    back_pieces()
    t = [s["news"][k].astype(F32) for k in range(Z)]
    for i in range(HIGH):
        a = pltpu.roll(t[i], ROWS - i, 1) if i else t[i]
        tile = jnp.where(rows_of(a) < HIGH - i, a, pltpu.roll(t[i + 1], HIGH - i, 1)).astype(BF16)
        O["A"][(*own["A"], i)] = tile[:LEFT]
        O["C"][(*own["C"], i)] = tile[LEFT:]
    for i in range(2):
        few.arrive(s["news_low"].at[i], low + i)
    a, b = ([s["news_low"][i, j].astype(F32) for j in range(3)] for i in range(2))
    seam = jnp.where(rows_of(b[0]) < ROWS // 2, a[2], pltpu.roll(b[0], ROWS // 2, 1))
    for i, tile in enumerate((a[0], a[1], seam, *(joined(b[j], b[j + 1], ROWS // 2) for j in range(2)))):
        O["B"][(*own["B"], i)] = tile.astype(BF16)

    gather = Gather(p, O, g_sent, g_arrived)
    for n, t in enumerate(GATHER_ORDER):
        gather.send(t)
        if 2 * n == len(GATHER_ORDER):

            @pl.loop(0, 2 * HALF)
            def _(c):
                for i in range(2):
                    for w in range(2):
                        for layer in range(LAYERS):
                            rows = pl.ds(LAYERS * c + layer, HIGH, stride=LAYERS * 2 * HALF)
                            made[3 * i + w][rows, :] = s["mv"][i, w, layer, c, pl.ds(0, HIGH)]

            @pl.loop(0, HIGH)
            def _(c):
                for i in range(2):
                    for layer in range(LAYERS):
                        for j, k in enumerate(DOWN_ROWS):
                            rows = pl.ds(ROWS * j * LAYERS * HIGH + LAYERS * c + layer, k, stride=LAYERS * HIGH)
                            made[3 * i + 2][rows, :] = s["mv_low"][i, layer, j, c, pl.ds(0, k)]

            for one in [reduce.copy(t) for t in REDUCE] + few.pushed:
                one.wait_send()
    for t in GATHER_ORDER:
        gather.wait(t)
    for t in GATHER:
        gather.copy(t).wait_send()


def put(*refs):
    (a, b, c), moments, (gate, up, down), results, sem = refs[:3], refs[3:9], refs[9:12], refs[12:18], refs[18]
    pairs = list(zip(moments, results))
    for z in range(Z):
        ref, layer, half = (gate, up)[z // X], z // 2 % 2, z % 2
        pairs.append((a.at[:, :, z], ref.at[layer, :, :, :, half, pl.ds(0, LEFT)]))
        pairs.append((c.at[z], ref.at[layer, :, :, :, half, pl.ds(LEFT, HALF - LEFT)]))
        layer, q = down_place(z)
        pairs += [(b.at[y, z], down.at[layer, :, y, q]) for y in range(Y)]
    copies = [pltpu.make_async_copy(src, dst, sem.at[i]) for i, (src, dst) in enumerate(pairs)]
    for one in copies:
        one.start()
    for one in copies:
        one.wait()


def tiled(a, *cut):
    rows, columns = cut
    n = len(rows)
    a = a.reshape(LAYERS, *rows, ROWS, *columns, LANES)
    order = [*range(n + 1), *range(n + 2, n + 2 + len(columns)), n + 1, a.ndim - 1]
    return a.transpose(order)


def untiled(a, *cut):
    rows, columns = cut
    n = len(rows)
    order = [*range(n + 1), a.ndim - 2, *range(n + 1, a.ndim - 2), a.ndim - 1]
    a = a.transpose(order)
    return a.reshape(LAYERS, -1, a.shape[-1] * (HALF * 2 if len(columns) == 2 else HIGH))


WIDE, TALL = ((X, Y, HIGH), (2, HALF)), ((X, Y, X, PART), (HIGH,))


def unmoment(a, rows, columns):
    return a.reshape(rows, columns, LAYERS, LANES).transpose(0, 2, 1, 3).reshape(rows, LAYERS, columns * LANES).transpose(1, 0, 2)


def solution(mesh):
    shapes = [pltpu.VMEM((*lens(c), *BLOCK[c], *TILE), BF16) for c in COLOURS]
    hbm, vmem = pl.BlockSpec(memory_space=pltpu.HBM), pl.BlockSpec(memory_space=pltpu.VMEM)
    moment = (LAYERS * HIGH * HALF * 2, LANES)

    def semaphores(n):
        return pltpu.SemaphoreType.DMA((n,))

    def kernel(body, name, params, **more):
        return pl.pallas_call(body, name=name, compiler_params=pltpu.CompilerParams(**params), **more)

    def step(*arrays):
        terms, weights, moments = [t[0] for t in arrays[:3]], arrays[3:6], arrays[6:]
        wide = [tiled(a, *WIDE) for a in (*terms[:2], *weights[:2])]
        operands = [*wide[:2], tiled(terms[2], *TALL), *wide[2:], tiled(weights[2], (FF // ROWS,), (HIGH,))]
        operands += [a.transpose(1, 0, 2) for a in moments]
        made = kernel(
            work,
            "work",
            dict(collective_id=0, has_side_effects=True, vmem_limit_bytes=34 << 20),
            out_shape=(*shapes, *[pltpu.VMEM(moment, F32)] * 6),
            in_specs=[hbm] * 12,
            out_specs=[vmem] * 9,
            scratch_shapes=[
                *shapes,
                *(pltpu.VMEM(*a) for a in SCRATCH.values()),
                *(semaphores(lens(c)[0]) for c in COLOURS),
                semaphores(16),
                *(semaphores(n) for n in (len(REDUCE), len(REDUCE), len(GATHER), len(GATHER), 64, 64)),
            ],
        )(*(pltpu.with_memory_space_constraint(a, pltpu.HBM) for a in operands))
        out = kernel(
            put,
            "put",
            dict(vmem_limit_bytes=1 << 20),
            out_shape=[jax.ShapeDtypeStruct(a.shape, BF16) for a in operands[:3]] + [jax.ShapeDtypeStruct(moment, F32)] * 6,
            in_specs=[vmem] * 9,
            out_specs=[hbm] * 9,
            scratch_shapes=[semaphores(54)],
        )(*made)
        weights = [untiled(a, *cut) for a, cut in zip(out, (WIDE, WIDE, TALL))]
        return (*weights, *(unmoment(a, *m.shape[1:2], m.shape[2] // LANES) for a, m in zip(out[3:], moments)))

    all_of, cut = P(None, None, None), P(None, "dp", None)
    return jax.shard_map(
        step,
        mesh=mesh,
        in_specs=(P(("rep", "dp"), None, None, None),) * 3 + (all_of,) * 3 + (cut,) * 6,
        out_specs=(P("rep", None, None),) * 3 + (P("rep", "dp", None),) * 6,
        check_vma=False,
    )
```

time: 1300 us -> 252 us (0.19)
  waiting for transfers between devices: 840 us -> 0 us
  blocking collectives: 308 us -> 0 us
  Pallas kernels: 0 us -> 250 us
  local copies, waits for them, and re-layouts: 122 us -> 0 us
  between operations: 17.9 us -> 0.65 us
    unnamed x5 -> x0, waiting for transfers between devices: 452 us -> none
    all_gather x3 -> x0, waiting for transfers between devices: 388 us -> none  [step(): whole = [lax.all_gather(one[0], 'dp', axis=1, tiled=True) for one in new]]
    psum x1 -> x0, blocking collectives: 308 us -> none  [step(): squares = lax.psum(sum((jnp.sum(g * g) for g in gradients)), 'dp')]
    pallas_call x0 -> x2, Pallas kernels: none -> 250 us  [the longest x1 240 us: step(): kernel(work, 'work', dict(collective_id=0, has_side_effects=True, vmem_li...]
    unnamed x29 -> x0, local copies, waits for them, and re-layouts: 120 us -> none
  transfers between devices with their start and end apart: 4 -> 0, of which waited for: 4 -> 0; matrix products, arithmetic and copies ran while one was open for 2% -> 0% of each run, Pallas kernels for 0% -> 0%
where the time goes in v1:
time: 252 us; the launch traced here: 251 us
  Pallas kernels  250 us (99%)
    pallas_call x1, Pallas kernels, step(): kernel(work, 'work', dict(collective_id=0, has_side_effects=True, vmem_li...  240 us
    pallas_call x1, Pallas kernels, step(): kernel(put, 'put', dict(vmem_limit_bytes=1 << 20), out_shape=[jax.ShapeDt...  9.75 us

profile of v1, /device:TPU:2, one launch (start us, length us, event | category | flops | bytes accessed | tf_op | source)
XLA Modules:
  0.0 250.5 jit_solution(16399002919253344143)
XLA Ops:
  0.6 240.1 %work.1 = (bf16[4,4,8,7,6,8,128]{6,5,4,3,2,1,0:T(8,128)(2,1)S(1)}, bf16[4,8,4,5,7,8,128]{6,5,4,3,2,1,0:T(8,128)(2,1)S(1)}, bf16[8,4,4,7,4,8,128]{6,5,4,3,2,1,0:T...) custom-call(bf16[2,4,4,7,2,10,8,128]{7,6,5,4,3,2,1,0:T(8,128)(2,1)} , ...), custom_call_target="tpu_custom_call" | custom-call | tf_op jit(solution)/shard_map/work/pallas_call | solution.py:610
  240.8 9.8 %put.1 = (bf16[2,4,4,7,2,10,8,128]{7,6,5,4,3,2,1,0:T(8,128)(2,1)}, bf16[2,4,4,7,2,10,8,128]{7,6,5,4,3,2,1,0:T(8,128)(2,1)}, bf16[2,4,4,4,5,7,8,128]{7,6,5,4,3,2,...) custom-call(bf16[4,4,8,7,6,8,128]{6,5,4,3,2,1,0:T(8,128)(2,1)S(1)} %, ...), custom_call_target="tpu_custom_call" | custom-call | tf_op jit(solution)/shard_map/put/pallas_call | solution.py:625

commit v2 on v1

--- a/solution.py
+++ b/solution.py
@@ -1,3 +1,5 @@
+import functools
+
 import jax
 import jax.numpy as jnp
 from jax import lax
@@ -28,7 +30,7 @@
 
 
 def down_place(z):
-    return (0, (z + 1) // 2 % X) if z % 2 else (1, (z // 2 + 3) % X)
+    return z % 2, z // 2
 
 
 def ring(n, ant):
@@ -95,7 +97,8 @@
         ready = [
             t
             for t in left
-            if all(arrives.get(w, now + 1) <= now for w in messages[t][2]) and 2 * sum(q[1] for q in queues[messages[t][0]]) <= slack
+            if all(arrives.get(w, now + 1) <= now for w in messages[t][2])
+            and 2 * sum(q[1] for q in queues[messages[t][0]]) <= slack
         ]
         if ready:
             t = max(ready, key=way)
@@ -130,7 +133,15 @@
         REDUCE[back(w)][2].append(back(t))
 REDUCE_ORDER = [back(t) for t in reversed(ENDS)]
 R_ID = {t: i for i, t in enumerate(REDUCE)}
-G_ID = {t: i for i, t in enumerate(GATHER)}
+G_ID = {t: R_ID[back(t)] for t in GATHER}
+S_ID = {t: i for i, t in enumerate((c, phase) for c in COLOURS for phase in range(1, 4))}
+
+
+def all_sent(T, sem):
+    for (c, phase), i in S_ID.items():
+        n = lens(c)[phase - 1] - 1
+        ref = T[c].at[(*[0] * (phase - 1), pl.ds(0, n))]
+        pltpu.make_async_copy(ref, ref, sem.at[i]).wait()
 
 
 class Place:
@@ -151,10 +162,8 @@
         self.device = device
         self.beside = {(d, e): device(**{d: self.offset[d, e]}) for d in SIZE for e in (1, -1)}
         self.line = [ahead("z", k) for k in range(Z)]
-        self.line_from = [ahead("z", -k) for k in range(Z)]
         self.line_device = [device(z=to) for to in self.line]
         self.plane_device = [device(x=ahead("x", k // Y), y=ahead("y", k % Y)) for k in range(X * Y)]
-        self.plane_from = [Y * ahead("x", -(k // Y)) + ahead("y", -(k % Y)) for k in range(X * Y)]
 
     def off(self, dim, k):
         n = SIZE[dim]
@@ -170,37 +179,52 @@
     pl.semaphore_wait(barrier, len(peers))
 
 
-def start_loads(p, gate, up, down, T, sem):
-    for step in range(Z):
-        for c in COLOURS:
-            n1 = lens(c)[0]
-            if step >= n1:
-                continue
-            k = far_first(n1)[step]
-            j = p.off(DIMS[c][0], k)
-            s = sem[c].at[k % n1]
+class Loads:
+    def __init__(self, p, terms, T, sem):
+        self.p, self.terms, self.T, self.sem = p, terms, T, sem
+        self.waited, self.left = set(), []
+        for c, phase, _, d, k in REDUCE_ORDER:
+            group = (c, d * k % lens(c)[0])
+            if phase == 1 and group not in self.left:
+                self.left.append(group)
+        self.left += [(c, 0) for c in COLOURS]
+
+    def start(self, count):
+        p, (gate, up, down) = self.p, self.terms
+        for c, k in self.left[:count]:
+            j, T, s = p.off(DIMS[c][0], k), self.T[c], self.sem[c].at[k]
             if c == "A":
                 for z in range(Z):
                     src = (gate, up)[z // X].at[z // 2 % 2, j, :, :, z % 2, pl.ds(0, LEFT)]
-                    pltpu.make_async_copy(src, T[c].at[j, :, z], s).start()
+                    pltpu.make_async_copy(src, T.at[j, :, z], s).start()
             elif c == "B":
                 for z in range(Z):
                     layer, q = down_place(z)
-                    pltpu.make_async_copy(down.at[layer, :, j, q], T[c].at[j, z], s).start()
+                    pltpu.make_async_copy(down.at[layer, :, j, q], T.at[j, z], s).start()
             else:
                 layer, half = lax.rem(lax.div(j, 2), 2), lax.rem(j, 2)
 
                 def load(ref):
-                    pltpu.make_async_copy(ref.at[layer, :, :, :, half, pl.ds(LEFT, HALF - LEFT)], T[c].at[j], s).start()
+                    pltpu.make_async_copy(ref.at[layer, :, :, :, half, pl.ds(LEFT, HALF - LEFT)], T.at[j], s).start()
 
                 pl.when(j < X)(lambda: load(gate))
                 pl.when(j >= X)(lambda: load(up))
+        self.left = self.left[count:]
+
+    def wait(self, c, k):
+        k %= lens(c)[0]
+        if (c, k) not in self.waited:
+            self.waited.add((c, k))
+            ref = self.T[c].at[self.p.off(DIMS[c][0], k)]
+            pltpu.make_async_copy(ref, ref, self.sem[c].at[k]).wait()
+            self.start(2)
 
 
 class Reduce:
     def __init__(self, p, T, O, load, sent, arrived):
         self.p, self.T, self.O, self.load, self.sent, self.arrived = p, T, O, load, sent, arrived
-        self.waited, self.loaded = set(), set()
+        self.waited = set()
+
 
     def areas(self, t):
         c, phase, unit, d, k = t
@@ -224,7 +248,7 @@
         return pltpu.make_async_remote_copy(
             src_ref=self.T[c].at[(*src, pl.ds(i, n))],
             dst_ref=self.O[c].at[(*dst, pl.ds(j, n))],
-            send_sem=self.sent.at[s],
+            send_sem=self.sent.at[S_ID[c, phase]],
             recv_sem=self.arrived.at[s],
             device_id=self.p.beside[DIMS[c][phase - 1], d],
             device_id_type=MESH,
@@ -234,13 +258,6 @@
         if t not in self.waited:
             self.waited.add(t)
             self.copy(t).wait_recv()
-
-    def wait_load(self, c, k):
-        k %= lens(c)[0]
-        if (c, k) not in self.loaded:
-            self.loaded.add((c, k))
-            ref = self.T[c].at[self.p.off(DIMS[c][0], k)]
-            pltpu.make_async_copy(ref, ref, self.load[c].at[k]).wait()
 
     def ended(self, c, phase, j2, j3):
         last = lens(c)[0] - 1
@@ -251,7 +268,7 @@
         T, O = self.T[c], self.O[c]
         for w in REDUCE[t][2]:
             self.wait(w)
-        self.wait_load(c, d * k if phase == 1 else 0)
+        self.load.wait(c, d * k if phase == 1 else 0)
         src, first, _, _, count = self.areas(t)
         before = (c, phase, unit, d, k + 1)
         chain = before in R_ID
@@ -278,7 +295,7 @@
         for t in REDUCE:
             if t[0] == c and t[-1] == 1 and t[2] in ((), (0,), (0, 0)):
                 self.wait(t)
-        self.wait_load(c, 0)
+        self.load.wait(c, 0)
         i, j, k = (self.p.at[d] for d in DIMS[c])
         total = self.T[c][i, j, k].astype(F32)
         for part in self.ended(c, 3, j, k) + [(n1 - 1, n2 - 1, e) for e in (0, 1)]:
@@ -302,7 +319,12 @@
             at = (p.at[d1], behind, p.off(d3, unit[0])) if phase == 2 else (p.at[d1], p.at[d2], behind)
         ref, s = self.O[c].at[at], G_ID[t]
         return pltpu.make_async_remote_copy(
-            src_ref=ref, dst_ref=ref, send_sem=self.sent.at[s], recv_sem=self.arrived.at[s], device_id=p.beside[dim, d], device_id_type=MESH
+            src_ref=ref,
+            dst_ref=ref,
+            send_sem=self.sent.at[S_ID[c, phase]],
+            recv_sem=self.arrived.at[s],
+            device_id=p.beside[dim, d],
+            device_id_type=MESH,
         )
 
     def wait(self, t):
@@ -334,6 +356,8 @@
 SCRATCH = {
     "raw": ((2, 2, HIGH, LAYERS, FF), F32),
     "raw_down": ((2, 20, LAYERS, D), F32),
+    "own": ((HIGH, HALF, *TILE), F32),
+    "own_low": ((PART, HIGH, *TILE), F32),
     "old": ((2, LAYERS, 2, 2, HALF, *TILE), BF16),
     "old_down": ((LAYERS, 3, HIGH, *TILE), BF16),
     "w": ((2, LAYERS, 2 * HALF, *TILE), F32),
@@ -355,33 +379,25 @@
 
 class Few:
     def __init__(self, p, sent, arrived):
-        self.p, self.sent, self.arrived, self.pushed, self.used = p, sent, arrived, [], 0
-
-    def places(self, n):
-        self.used += n
-        return self.used - n
-
-    def push(self, src, dst, i, j, to):
-        one = pltpu.make_async_remote_copy(
-            src_ref=src, dst_ref=dst, send_sem=self.sent.at[i], recv_sem=self.arrived.at[j], device_id=to, device_id_type=MESH
-        )
-        self.pushed.append(one)
-        one.start()
-
-    def arrive(self, ref, i):
-        pltpu.make_async_copy(ref, ref, self.arrived.at[i]).wait()
+        self.p, self.sent, self.arrived, self.waits = p, sent, arrived, []
+
+    def exchange(self, copies, get):
+        i = len(self.waits)
+        for src, dst, to in copies:
+            one = pltpu.make_async_remote_copy(
+                src_ref=src, dst_ref=dst, send_sem=self.sent.at[i], recv_sem=self.arrived.at[i], device_id=to, device_id_type=MESH
+            )
+            one.start()
+        self.waits.append(pltpu.make_async_copy(get, get, self.sent.at[i]).wait)
+        return pltpu.make_async_copy(get, get, self.arrived.at[i]).wait
 
     def line(self, out, into):
-        p, base = self.p, self.places(Z)
-        z = p.at["z"]
-        for k in range(1, Z):
-            self.push(out.at[p.line[k]], into.at[z], base + k, base + k, p.line_device[k])
-
-        def wait():
-            for k in range(1, Z):
-                self.arrive(into.at[p.line_from[k]], base + k)
-
-        return wait
+        p = self.p
+        far = sorted(range(1, Z), key=lambda k: abs(k - X))
+        return self.exchange([(out.at[p.line[k]], into.at[p.at["z"]], p.line_device[k]) for k in far], into.at[pl.ds(0, Z - 1)])
+
+    def tell(self, ref, at, devices):
+        return self.exchange([(ref.at[at], ref.at[at], to) for to in devices], ref.at[pl.ds(0, len(devices))])
 
 
 def lanes(c):
@@ -393,99 +409,113 @@
     outs, made, refs = refs[:3], refs[3:9], refs[9:]
     O, T, refs = dict(zip(COLOURS, outs)), dict(zip(COLOURS, refs)), refs[3:]
     s = dict(zip(SCRATCH, refs))
-    *load, small, r_sent, r_arrived, g_sent, g_arrived, x_sent, x_arrived = refs[len(SCRATCH) :]
+    *load, small, sent, arrived, few_sent, few_arrived = refs[len(SCRATCH) :]
     p = Place()
     x, y, z = p.at.values()
-    start_loads(p, *terms, T, dict(zip(COLOURS, load)))
-
-    plain = []
-
-    def fetch(src, dst):
-        plain.append(pltpu.make_async_copy(src, dst, small.at[len(plain)]))
-        plain[-1].start()
+    loads = Loads(p, terms, T, dict(zip(COLOURS, load)))
+    loads.start(4)
 
     first = (X * Y * PART) * x + 20 * y + lax.div(PART * z, 2)
     for layer in range(LAYERS):
         for w in range(2):
             for i, row in enumerate((lax.max(z - 1, 0), lax.min(z, HIGH - 1))):
-                fetch(weights[w].at[layer, x, y, row], s["old"].at[w, layer, i])
-        fetch(weights[2].at[layer, pl.ds(first, 3)], s["old_down"].at[layer])
+                pltpu.make_async_copy(weights[w].at[layer, x, y, row], s["old"].at[w, layer, i], small.at[0]).start()
+        pltpu.make_async_copy(weights[2].at[layer, pl.ds(first, 3)], s["old_down"].at[layer], small.at[1]).start()
     for i in range(2):
         for w in range(2):
-            fetch(moments[3 * i + w], s["raw"].at[i, w])
-        fetch(moments[3 * i + 2], s["raw_down"].at[i])
-
-    def unpack():
-        for one in plain:
-            one.wait()
-        for layer in range(LAYERS):
-            for w in range(2):
-                low, high = (s["old"][w, layer, i].reshape(2 * HALF, *TILE).astype(F32) for i in range(2))
-                s["w"][w, layer] = joined(low, high, z)
-            part = [s["old_down"][layer, j].astype(F32) for j in range(3)]
-            for j in range(3):
-                s["w_low"][layer, j] = jnp.where(lax.rem(z, 2) == 1, joined(part[j], part[min(j + 1, 2)], ROWS // 2), part[j])
-
+            pltpu.make_async_copy(moments[3 * i + w], s["raw"].at[i, w], small.at[2]).start()
+        pltpu.make_async_copy(moments[3 * i + 2], s["raw_down"].at[i], small.at[3]).start()
+
+    def rows_here():
+        for i, name in enumerate(("old", "old_down", "raw", "raw_down")):
+            pltpu.make_async_copy(s[name], s[name], small.at[i]).wait()
+
+    chores, later = [rows_here], []
+
+    def rows_in(w, layer):
+        low, high = (s["old"][w, layer, i].reshape(2 * HALF, *TILE).astype(F32) for i in range(2))
+        s["w"][w, layer] = joined(low, high, z)
+
+    def rows_in_low(layer):
+        part = [s["old_down"][layer, j].astype(F32) for j in range(3)]
+        for j in range(3):
+            s["w_low"][layer, j] = jnp.where(lax.rem(z, 2) == 1, joined(part[j], part[min(j + 1, 2)], ROWS // 2), part[j])
+
+    def moments_in(i, w, layer):
         @pl.loop(0, 2 * HALF)
         def _(c):
-            for i in range(2):
-                for w in range(2):
-                    for layer in range(LAYERS):
-                        s["mv"][i, w, layer, c, pl.ds(0, HIGH)] = s["raw"][i, w, :, layer, lanes(c)]
-
+            s["mv"][i, w, layer, c, pl.ds(0, HIGH)] = s["raw"][i, w, :, layer, lanes(c)]
+
+    def moments_in_low(i, layer):
         @pl.loop(0, HIGH)
         def _(c):
+            for j, n in enumerate(DOWN_ROWS):
+                s["mv_low"][i, layer, j, c, pl.ds(0, n)] = s["raw_down"][i, pl.ds(ROWS * j, n), layer, lanes(c)]
+
+    def moments_out(i, w, layer):
+        @pl.loop(0, 2 * HALF)
+        def _(c):
+            rows = pl.ds(LAYERS * c + layer, HIGH, stride=LAYERS * 2 * HALF)
+            made[3 * i + w][rows, :] = s["mv"][i, w, layer, c, pl.ds(0, HIGH)]
+
+    def moments_out_low(i, layer):
+        @pl.loop(0, HIGH)
+        def _(c):
+            for j, k in enumerate(DOWN_ROWS):
+                rows = pl.ds(ROWS * j * LAYERS * HIGH + LAYERS * c + layer, k, stride=LAYERS * HIGH)
+                made[3 * i + 2][rows, :] = s["mv_low"][i, layer, j, c, pl.ds(0, k)]
+
+    for layer in range(LAYERS):
+        for w in range(2):
+            chores.append(functools.partial(rows_in, w, layer))
             for i in range(2):
-                for layer in range(LAYERS):
-                    for j, n in enumerate(DOWN_ROWS):
-                        s["mv_low"][i, layer, j, c, pl.ds(0, n)] = s["raw_down"][i, pl.ds(ROWS * j, n), layer, lanes(c)]
+                chores.append(functools.partial(moments_in, i, w, layer))
+                later.append(functools.partial(moments_out, i, w, layer))
+        chores.append(functools.partial(rows_in_low, layer))
+        for i in range(2):
+            chores.append(functools.partial(moments_in_low, i, layer))
+            later.append(functools.partial(moments_out_low, i, layer))
 
     fence(p)
-    reduce = Reduce(p, T, O, dict(zip(COLOURS, load)), r_sent, r_arrived)
+    reduce = Reduce(p, T, O, loads, sent, arrived)
     for n, t in enumerate(REDUCE_ORDER):
-        if 2 * n == len(REDUCE_ORDER):
-            unpack()
         reduce.send(t)
-
-    few = Few(p, x_sent, x_arrived)
+        if n > len(REDUCE_ORDER) // 4 and n % 4 == 0 and chores:
+            chores.pop(0)()
+
+    few = Few(p, few_sent, few_arrived)
     squares = jnp.zeros(TILE, F32)
-    for c in ("C", "A"):
+    for c in COLOURS:
         g = reduce.own(c)
-        n = BLOCK[c][1]
-        place = pl.ds(0 if c == "A" else LEFT, n)
-        squares = squares + jnp.sum((g * g).reshape(HIGH * n, *TILE), axis=0)
-        for k in range(Z):
-            before, at = g[max(k - 1, 0)], g[min(k, HIGH - 1)]
-            s["out"][k, place] = (joined(before, at, k) if k else at).astype(BF16)
+        if c == "B":
+            s["own_low"][...] = g
+        else:
+            s["own"][:, pl.ds(*((0, LEFT) if c == "A" else (LEFT, HALF - LEFT)))] = g
+        squares = squares + jnp.sum((g * g).reshape(tiles(c), *TILE), axis=0)
+    s["z_sum"][z] = squares
+    line_sums = few.tell(s["z_sum"], z, p.line_device[1:])
+
+    for k in range(Z):
+        at = s["own"][min(k, HIGH - 1)]
+        s["out"][k] = (joined(s["own"][k - 1], at, k) if k else at).astype(BF16)
     pieces = few.line(s["out"], s["into"])
     s["into"][z] = s["out"][z]
-
-    g = reduce.own("B")
-    squares = squares + jnp.sum((g * g).reshape(PART * HIGH, *TILE), axis=0)
+    g = [s["own_low"][j] for j in range(PART)]
     for j in range(3):
         s["out_low"][0, j] = g[j].astype(BF16)
         s["out_low"][1, j] = joined(g[2 + j], g[min(3 + j, PART - 1)], ROWS // 2).astype(BF16)
-    my_layer = 1 - lax.rem(z, 2)
-    my_pair = lax.rem(lax.div(z + 1, 2) + 3 * my_layer, X)
-    low = few.places(2)
-    for i in range(2):
-        few.push(s["out_low"].at[i], s["into_low"].at[my_layer], low + i, low + my_layer, p.device(z=2 * my_pair + i))
-
-    base = few.places(Z)
-    s["z_sum"][z] = squares
-    for k in range(1, Z):
-        few.push(s["z_sum"].at[z], s["z_sum"].at[z], base + k, base + k, p.line_device[k])
-    for k in range(1, Z):
-        few.arrive(s["z_sum"].at[p.line_from[k]], base + k)
-    base, mine = few.places(X * Y), Y * x + y
-    s["sum"][mine] = jnp.sum(s["z_sum"][...], axis=0)
-    for k in range(1, X * Y):
-        few.push(s["sum"].at[mine], s["sum"].at[mine], base + k, base + k, p.plane_device[k])
+    mine = lax.rem(z, 2)
+    other, partner = 1 - mine, p.device(z=z + 1 - 2 * mine)
+    pieces_low = few.exchange([(s["out_low"].at[other], s["into_low"].at[mine], partner)], s["into_low"].at[other])
+    s["into_low"][mine] = s["out_low"][mine]
+
+    line_sums()
+    at = Y * x + y
+    s["sum"][at] = jnp.sum(s["z_sum"][...], axis=0)
+    sums = few.tell(s["sum"], at, p.plane_device[1:])
     pieces()
-    for layer in range(LAYERS):
-        few.arrive(s["into_low"].at[layer], low + layer)
-    for k in range(1, X * Y):
-        few.arrive(s["sum"].at[p.plane_from[k]], base + k)
+    pieces_low()
+    sums()
     total = jnp.sum(s["sum"][...], axis=0)
     total = jnp.sum(jnp.sum(total, axis=1, keepdims=True), axis=0, keepdims=True)
     factor = jnp.minimum(1.0, 0.5 * lax.rsqrt(total / COUNT + 1e-30))
@@ -496,76 +526,68 @@
         new, m, v = adamw(s["w"][w, layer, part], s["mv"][0, w, layer, part], s["mv"][1, w, layer, part], g)
         s["mv"][0, w, layer, part], s["mv"][1, w, layer, part] = m, v
         s["new"][owner] = new.astype(BF16)
-    back_pieces = few.line(s["new"], s["news"])
+    pieces = few.line(s["new"], s["news"])
     for layer in range(LAYERS):
         g = s["into_low"][layer].astype(F32) * factor
         new, m, v = adamw(s["w_low"][layer], s["mv_low"][0, layer], s["mv_low"][1, layer], g)
         s["mv_low"][0, layer], s["mv_low"][1, layer] = m, v
         s["new_low"][layer] = new.astype(BF16)
+    pieces_low = few.exchange([(s["new_low"].at[other], s["news_low"].at[mine], partner)], s["news_low"].at[other])
+    s["news_low"][mine] = s["new_low"][mine]
     s["news"][z] = s["new"][z]
-    low, parity = few.places(2), lax.rem(z, 2)
-    for layer in range(LAYERS):
-        to = lax.rem(z - parity + (Z - 1, 2)[layer], Z)
-        few.push(s["new_low"].at[layer], s["news_low"].at[parity], low + layer, low + parity, p.device(z=to))
 
     own = {c: tuple(p.at[d] for d in DIMS[c]) for c in COLOURS}
-    back_pieces()
-    t = [s["news"][k].astype(F32) for k in range(Z)]
-    for i in range(HIGH):
-        a = pltpu.roll(t[i], ROWS - i, 1) if i else t[i]
-        tile = jnp.where(rows_of(a) < HIGH - i, a, pltpu.roll(t[i + 1], HIGH - i, 1)).astype(BF16)
-        O["A"][(*own["A"], i)] = tile[:LEFT]
-        O["C"][(*own["C"], i)] = tile[LEFT:]
-    for i in range(2):
-        few.arrive(s["news_low"].at[i], low + i)
-    a, b = ([s["news_low"][i, j].astype(F32) for j in range(3)] for i in range(2))
-    seam = jnp.where(rows_of(b[0]) < ROWS // 2, a[2], pltpu.roll(b[0], ROWS // 2, 1))
-    for i, tile in enumerate((a[0], a[1], seam, *(joined(b[j], b[j + 1], ROWS // 2) for j in range(2)))):
-        O["B"][(*own["B"], i)] = tile.astype(BF16)
-
-    gather = Gather(p, O, g_sent, g_arrived)
+
+    def whole_low():
+        pieces_low()
+        a, b = ([s["news_low"][i, j].astype(F32) for j in range(3)] for i in range(2))
+        seam = jnp.where(rows_of(b[0]) < ROWS // 2, a[2], pltpu.roll(b[0], ROWS // 2, 1))
+        for i, tile in enumerate((a[0], a[1], seam, *(joined(b[j], b[j + 1], ROWS // 2) for j in range(2)))):
+            O["B"][(*own["B"], i)] = tile.astype(BF16)
+
+    def whole():
+        pieces()
+        t = [s["news"][k].astype(F32) for k in range(Z)]
+        for i in range(HIGH):
+            a = pltpu.roll(t[i], ROWS - i, 1) if i else t[i]
+            tile = jnp.where(rows_of(a) < HIGH - i, a, pltpu.roll(t[i + 1], HIGH - i, 1)).astype(BF16)
+            O["A"][(*own["A"], i)] = tile[:LEFT]
+            O["C"][(*own["C"], i)] = tile[LEFT:]
+
+    all_sent(T, sent)
+    gather = Gather(p, O, sent, arrived)
+    prepare = {"B": whole_low, "A": whole}
     for n, t in enumerate(GATHER_ORDER):
+        needs = "B" if t[0] == "B" else "A"
+        if needs in prepare:
+            prepare.pop(needs)()
         gather.send(t)
-        if 2 * n == len(GATHER_ORDER):
-
-            @pl.loop(0, 2 * HALF)
-            def _(c):
-                for i in range(2):
-                    for w in range(2):
-                        for layer in range(LAYERS):
-                            rows = pl.ds(LAYERS * c + layer, HIGH, stride=LAYERS * 2 * HALF)
-                            made[3 * i + w][rows, :] = s["mv"][i, w, layer, c, pl.ds(0, HIGH)]
-
-            @pl.loop(0, HIGH)
-            def _(c):
-                for i in range(2):
-                    for layer in range(LAYERS):
-                        for j, k in enumerate(DOWN_ROWS):
-                            rows = pl.ds(ROWS * j * LAYERS * HIGH + LAYERS * c + layer, k, stride=LAYERS * HIGH)
-                            made[3 * i + 2][rows, :] = s["mv_low"][i, layer, j, c, pl.ds(0, k)]
-
-            for one in [reduce.copy(t) for t in REDUCE] + few.pushed:
-                one.wait_send()
-    for t in GATHER_ORDER:
+        if n > len(GATHER_ORDER) // 4 and n % 4 == 0 and later:
+            later.pop(0)()
+    for t in ENDS:
         gather.wait(t)
-    for t in GATHER:
-        gather.copy(t).wait_send()
+    for wait in few.waits:
+        wait()
+    all_sent(T, sent)
 
 
 def put(*refs):
-    (a, b, c), moments, (gate, up, down), results, sem = refs[:3], refs[3:9], refs[9:12], refs[12:18], refs[18]
-    pairs = list(zip(moments, results))
+    (a, b, c), moments, results, sem = refs[:3], refs[3:9], refs[9:18], refs[18]
+
+    def copy(src, i, *at):
+        pltpu.make_async_copy(src, results[i].at[at] if at else results[i], sem.at[i]).start()
+
     for z in range(Z):
-        ref, layer, half = (gate, up)[z // X], z // 2 % 2, z % 2
-        pairs.append((a.at[:, :, z], ref.at[layer, :, :, :, half, pl.ds(0, LEFT)]))
-        pairs.append((c.at[z], ref.at[layer, :, :, :, half, pl.ds(LEFT, HALF - LEFT)]))
+        half, layer = z % 2, z // 2 % 2
+        copy(a.at[:, :, z], z // X, layer, slice(None), slice(None), slice(None), half, pl.ds(0, LEFT))
+        copy(c.at[z], z // X, layer, slice(None), slice(None), slice(None), half, pl.ds(LEFT, HALF - LEFT))
         layer, q = down_place(z)
-        pairs += [(b.at[y, z], down.at[layer, :, y, q]) for y in range(Y)]
-    copies = [pltpu.make_async_copy(src, dst, sem.at[i]) for i, (src, dst) in enumerate(pairs)]
-    for one in copies:
-        one.start()
-    for one in copies:
-        one.wait()
+        for y in range(Y):
+            copy(b.at[y, z], 2, layer, slice(None), y, q)
+    for i, moment in enumerate(moments):
+        copy(moment, 3 + i)
+    for i, ref in enumerate(results):
+        pltpu.make_async_copy(ref, ref, sem.at[i]).wait()
 
 
 def tiled(a, *cut):
@@ -618,8 +640,8 @@
                 *shapes,
                 *(pltpu.VMEM(*a) for a in SCRATCH.values()),
                 *(semaphores(lens(c)[0]) for c in COLOURS),
-                semaphores(16),
-                *(semaphores(n) for n in (len(REDUCE), len(REDUCE), len(GATHER), len(GATHER), 64, 64)),
+                semaphores(4),
+                *(semaphores(n) for n in (len(S_ID), len(R_ID), 6, 6)),
             ],
         )(*(pltpu.with_memory_space_constraint(a, pltpu.HBM) for a in operands))
         out = kernel(
@@ -629,7 +651,7 @@
             out_shape=[jax.ShapeDtypeStruct(a.shape, BF16) for a in operands[:3]] + [jax.ShapeDtypeStruct(moment, F32)] * 6,
             in_specs=[vmem] * 9,
             out_specs=[hbm] * 9,
-            scratch_shapes=[semaphores(54)],
+            scratch_shapes=[semaphores(9)],
         )(*made)
         weights = [untiled(a, *cut) for a, cut in zip(out, (WIDE, WIDE, TALL))]
         return (*weights, *(unmoment(a, *m.shape[1:2], m.shape[2] // LANES) for a, m in zip(out[3:], moments)))

time: 252 us -> 242 us (0.960)
  Pallas kernels: 250 us -> 240 us
    pallas_call x1, Pallas kernels: 240 us -> 231 us  [step(): kernel(work, 'work', dict(collective_id=0, has_side_effects=True, vmem_li...]
where the time goes in v2:
time: 242 us; the launch traced here: 241 us
  Pallas kernels  240 us (99%)
    pallas_call x1, Pallas kernels, step(): kernel(work, 'work', dict(collective_id=0, has_side_effects=True, vmem_li...  231 us
    pallas_call x1, Pallas kernels, step(): kernel(put, 'put', dict(vmem_limit_bytes=1 << 20), out_shape=[jax.ShapeDt...  9.37 us

profile of v2, /device:TPU:2, one launch (start us, length us, event | category | flops | bytes accessed | tf_op | source)
XLA Modules:
  0.0 241.0 jit_solution(14751512680850605421)
XLA Ops:
  0.6 231.0 %work.1 = (bf16[4,4,8,7,6,8,128]{6,5,4,3,2,1,0:T(8,128)(2,1)S(1)}, bf16[4,8,4,5,7,8,128]{6,5,4,3,2,1,0:T(8,128)(2,1)S(1)}, bf16[8,4,4,7,4,8,128]{6,5,4,3,2,1,0:T...) custom-call(bf16[2,4,4,7,2,10,8,128]{7,6,5,4,3,2,1,0:T(8,128)(2,1)} , ...), custom_call_target="tpu_custom_call" | custom-call | tf_op jit(solution)/shard_map/work/pallas_call | solution.py:632
  231.6 9.4 %put.1 = (bf16[2,4,4,7,2,10,8,128]{7,6,5,4,3,2,1,0:T(8,128)(2,1)}, bf16[2,4,4,7,2,10,8,128]{7,6,5,4,3,2,1,0:T(8,128)(2,1)}, bf16[2,4,4,4,5,7,8,128]{7,6,5,4,3,2,...) custom-call(bf16[4,4,8,7,6,8,128]{6,5,4,3,2,1,0:T(8,128)(2,1)S(1)} %, ...), custom_call_target="tpu_custom_call" | custom-call | tf_op jit(solution)/shard_map/put/pallas_call | solution.py:647

commit v3 on v2

--- a/solution.py
+++ b/solution.py
@@ -58,6 +58,9 @@
     return (c, phase, unit, 1, n - o) if far else (c, phase, unit, -1, o)
 
 
+SECOND_BY_BLOCK, FIRST_BY_BLOCK = "AB", "A"
+
+
 def gather_messages():
     out = {}
     for c in COLOURS:
@@ -68,13 +71,15 @@
             for d, k in ring(SIZE[dim], ant_in(phase, unit)):
                 out[c, phase, unit, d, k] = ((dim, d), count * tiles(c), [(c, phase, unit, d, k - 1)] if k > 1 else first)
 
+        blocks, whole = [(o,) for o in range(n3)], [(None,)]
         add(3, (), 1, [])
-        for o in range(n3):
-            first = [came(c, 3, (), n3, o)] if o else []
-            add(2, (o,), 1, first)
-            add(1, (0, o), 1, first)
+        line = [came(c, 3, (), n3, o) for o in range(1, n3)]
+        second = blocks if c in SECOND_BY_BLOCK else whole
+        for phase, head, chosen in ((2, (), second), (1, (0,), blocks if c in FIRST_BY_BLOCK else whole)):
+            for unit in chosen:
+                add(phase, head + unit, 1 if unit[0] is not None else n3, line[unit[0] - 1 : unit[0]] if unit[0] is not None else line)
         for o in range(1, n2):
-            add(1, (o, None), n3, [came(c, 2, (i,), n2, o) for i in range(n3)])
+            add(1, (o, None), n3, [came(c, 2, unit, n2, o) for unit in second])
     return out
 
 
@@ -115,11 +120,13 @@
             queues[link][0][1] -= pause * s
             if queues[link][0][1] <= 0:
                 arrives[queues[link].pop(0)[0]] = now + latency
-    return starts, list(arrives), arrives
+    return starts, list(arrives)
 
 
 GATHER = gather_messages()
-GATHER_ORDER, ENDS, GATHER_AT = ordered(GATHER, 2.0, 2.0, 43.0)
+GATHER_ORDER = ordered(GATHER, 1.0, 2.0, 60.0)[0]
+ENDS = ordered(GATHER, 0.5, 3.0, 50.0)[1]
+TURN = 67
 
 
 def back(t):
@@ -159,7 +166,7 @@
         def ahead(d, k):
             return lax.rem(at[d] + SIZE[d] + k, SIZE[d])
 
-        self.device = device
+        self.rep, self.device, self.twin = rep, device, (1 - rep, dp)
         self.beside = {(d, e): device(**{d: self.offset[d, e]}) for d in SIZE for e in (1, -1)}
         self.line = [ahead("z", k) for k in range(Z)]
         self.line_device = [device(z=to) for to in self.line]
@@ -171,12 +178,12 @@
         return self.offset[dim, k] if k else self.at[dim]
 
 
-def fence(p):
-    peers = p.line_device[1:] + p.plane_device[1:]
+def greet(p):
+    peers = [*p.beside.values(), p.twin]
     barrier = pltpu.get_barrier_semaphore()
     for peer in peers:
         pl.semaphore_signal(barrier, inc=1, device_id=peer, device_id_type=MESH)
-    pl.semaphore_wait(barrier, len(peers))
+    return lambda: pl.semaphore_wait(barrier, len(peers))
 
 
 class Loads:
@@ -237,8 +244,8 @@
             first, count = (0, n3) if unit[1] is None else (p.off(d3, unit[1]), 1)
             return (p.off(d1, d * k), j2), first, (slot, j2), first, count
         if phase == 2:
-            j3 = p.off(d3, unit[0])
-            return (p.at[d1], p.off(d2, d * k)), j3, (n1 - 1, slot), j3, 1
+            first, count = (0, n3) if unit[0] is None else (p.off(d3, unit[0]), 1)
+            return (p.at[d1], p.off(d2, d * k)), first, (n1 - 1, slot), first, count
         return (p.at[d1], p.at[d2]), p.off(d3, d * k), (n1 - 1, n2 - 1), slot, 1
 
     def copy(self, t):
@@ -293,7 +300,7 @@
     def own(self, c):
         n1, n2, _ = lens(c)
         for t in REDUCE:
-            if t[0] == c and t[-1] == 1 and t[2] in ((), (0,), (0, 0)):
+            if t[0] == c and t[-1] == 1 and not any(t[2]):
                 self.wait(t)
         self.load.wait(c, 0)
         i, j, k = (self.p.at[d] for d in DIMS[c])
@@ -313,10 +320,8 @@
         d1, d2, d3 = DIMS[c]
         p, dim = self.p, DIMS[c][phase - 1]
         behind = p.off(dim, d * (1 - came - k))
-        if phase == 1:
-            at = (behind, p.off(d2, unit[0])) if unit[1] is None else (behind, p.off(d2, unit[0]), p.off(d3, unit[1]))
-        else:
-            at = (p.at[d1], behind, p.off(d3, unit[0])) if phase == 2 else (p.at[d1], p.at[d2], behind)
+        at = (behind, p.off(d2, unit[0])) if phase == 1 else (p.at[d1], behind) if phase == 2 else (p.at[d1], p.at[d2], behind)
+        at += tuple(p.off(d3, o) for o in unit[-1:] if o is not None)
         ref, s = self.O[c].at[at], G_ID[t]
         return pltpu.make_async_remote_copy(
             src_ref=ref,
@@ -409,28 +414,30 @@
     outs, made, refs = refs[:3], refs[3:9], refs[9:]
     O, T, refs = dict(zip(COLOURS, outs)), dict(zip(COLOURS, refs)), refs[3:]
     s = dict(zip(SCRATCH, refs))
-    *load, small, sent, arrived, few_sent, few_arrived = refs[len(SCRATCH) :]
+    *load, small, turn, sent, arrived, few_sent, few_arrived = refs[len(SCRATCH) :]
     p = Place()
     x, y, z = p.at.values()
+    all_here = greet(p)
     loads = Loads(p, terms, T, dict(zip(COLOURS, load)))
     loads.start(4)
 
-    first = (X * Y * PART) * x + 20 * y + lax.div(PART * z, 2)
-    for layer in range(LAYERS):
-        for w in range(2):
-            for i, row in enumerate((lax.max(z - 1, 0), lax.min(z, HIGH - 1))):
-                pltpu.make_async_copy(weights[w].at[layer, x, y, row], s["old"].at[w, layer, i], small.at[0]).start()
-        pltpu.make_async_copy(weights[2].at[layer, pl.ds(first, 3)], s["old_down"].at[layer], small.at[1]).start()
-    for i in range(2):
-        for w in range(2):
-            pltpu.make_async_copy(moments[3 * i + w], s["raw"].at[i, w], small.at[2]).start()
-        pltpu.make_async_copy(moments[3 * i + 2], s["raw_down"].at[i], small.at[3]).start()
+    def rows_fetch():
+        first = (X * Y * PART) * x + 20 * y + lax.div(PART * z, 2)
+        for layer in range(LAYERS):
+            for w in range(2):
+                for i, row in enumerate((lax.max(z - 1, 0), lax.min(z, HIGH - 1))):
+                    pltpu.make_async_copy(weights[w].at[layer, x, y, row], s["old"].at[w, layer, i], small.at[0]).start()
+            pltpu.make_async_copy(weights[2].at[layer, pl.ds(first, 3)], s["old_down"].at[layer], small.at[1]).start()
+        for i in range(2):
+            for w in range(2):
+                pltpu.make_async_copy(moments[3 * i + w], s["raw"].at[i, w], small.at[2]).start()
+            pltpu.make_async_copy(moments[3 * i + 2], s["raw_down"].at[i], small.at[3]).start()
 
     def rows_here():
         for i, name in enumerate(("old", "old_down", "raw", "raw_down")):
             pltpu.make_async_copy(s[name], s[name], small.at[i]).wait()
 
-    chores, later = [rows_here], []
+    chores, later = [rows_fetch, rows_here], []
 
     def rows_in(w, layer):
         low, high = (s["old"][w, layer, i].reshape(2 * HALF, *TILE).astype(F32) for i in range(2))
@@ -476,10 +483,13 @@
             chores.append(functools.partial(moments_in_low, i, layer))
             later.append(functools.partial(moments_out_low, i, layer))
 
-    fence(p)
+    all_here()
     reduce = Reduce(p, T, O, loads, sent, arrived)
+    pl.when(p.rep == 0)(lambda: pl.semaphore_wait(turn, 1))
     for n, t in enumerate(REDUCE_ORDER):
         reduce.send(t)
+        if n == TURN:
+            pl.when(p.rep == 1)(lambda: pl.semaphore_signal(turn, inc=1, device_id=p.twin, device_id_type=MESH))
         if n > len(REDUCE_ORDER) // 4 and n % 4 == 0 and chores:
             chores.pop(0)()
 
@@ -641,6 +651,7 @@
                 *(pltpu.VMEM(*a) for a in SCRATCH.values()),
                 *(semaphores(lens(c)[0]) for c in COLOURS),
                 semaphores(4),
+                pltpu.SemaphoreType.REGULAR,
                 *(semaphores(n) for n in (len(S_ID), len(R_ID), 6, 6)),
             ],
         )(*(pltpu.with_memory_space_constraint(a, pltpu.HBM) for a in operands))

time: 242 us -> 230 us (0.950)
  Pallas kernels: 240 us -> 229 us
    pallas_call x1, Pallas kernels: 231 us -> 219 us  [step(): kernel(work, 'work', dict(collective_id=0, has_side_effects=True, vmem_li...]
where the time goes in v3:
time: 230 us
  Pallas kernels  229 us (100%)
    pallas_call x1, Pallas kernels, step(): kernel(work, 'work', dict(collective_id=0, has_side_effects=True, vmem_li...  219 us
    pallas_call x1, Pallas kernels, step(): kernel(put, 'put', dict(vmem_limit_bytes=1 << 20), out_shape=[jax.ShapeDt...  9.37 us

profile of v3, /device:TPU:2, one launch (start us, length us, event | category | flops | bytes accessed | tf_op | source)
XLA Modules:
  0.0 229.5 jit_solution(9848233817407930413)
XLA Ops:
  0.6 219.5 %work.1 = (bf16[4,4,8,7,6,8,128]{6,5,4,3,2,1,0:T(8,128)(2,1)S(1)}, bf16[4,8,4,5,7,8,128]{6,5,4,3,2,1,0:T(8,128)(2,1)S(1)}, bf16[8,4,4,7,4,8,128]{6,5,4,3,2,1,0:T...) custom-call(bf16[2,4,4,7,2,10,8,128]{7,6,5,4,3,2,1,0:T(8,128)(2,1)} , ...), custom_call_target="tpu_custom_call" | custom-call | tf_op jit(solution)/shard_map/work/pallas_call | solution.py:642
  220.1 9.4 %put.1 = (bf16[2,4,4,7,2,10,8,128]{7,6,5,4,3,2,1,0:T(8,128)(2,1)}, bf16[2,4,4,7,2,10,8,128]{7,6,5,4,3,2,1,0:T(8,128)(2,1)}, bf16[2,4,4,4,5,7,8,128]{7,6,5,4,3,2,...) custom-call(bf16[4,4,8,7,6,8,128]{6,5,4,3,2,1,0:T(8,128)(2,1)S(1)} %, ...), custom_call_target="tpu_custom_call" | custom-call | tf_op jit(solution)/shard_map/put/pallas_call | solution.py:658

commit v4 on v3

--- a/solution.py
+++ b/solution.py
@@ -124,9 +124,10 @@
 
 
 GATHER = gather_messages()
-GATHER_ORDER = ordered(GATHER, 1.0, 2.0, 60.0)[0]
+GATHER_ORDER, GATHER_ENDS = ordered(GATHER, 1.0, 2.0, 60.0)
 ENDS = ordered(GATHER, 0.5, 3.0, 50.0)[1]
 TURN = 67
+AHEAD = 12
 
 
 def back(t):
@@ -186,45 +187,48 @@
     return lambda: pl.semaphore_wait(barrier, len(peers))
 
 
+def block_of(t):
+    c, phase, unit, d, k = t
+    n1, n2, _ = lens(c)
+    return (c, d * k % n1, unit[0] % n2) if phase == 1 else (c, 0, d * k % n2 if phase == 2 else 0)
+
+
 class Loads:
     def __init__(self, p, terms, T, sem):
         self.p, self.terms, self.T, self.sem = p, terms, T, sem
-        self.waited, self.left = set(), []
-        for c, phase, _, d, k in REDUCE_ORDER:
-            group = (c, d * k % lens(c)[0])
-            if phase == 1 and group not in self.left:
-                self.left.append(group)
-        self.left += [(c, 0) for c in COLOURS]
+        self.left = list(dict.fromkeys([block_of(t) for t in REDUCE_ORDER] + [(c, 0, 0) for c in COLOURS]))
+        self.place = {part: i % AHEAD for i, part in enumerate(self.left)}
+
+    def at(self, part):
+        c, k, o = part
+        return self.p.off(DIMS[c][0], k), self.p.off(DIMS[c][1], o)
 
     def start(self, count):
-        p, (gate, up, down) = self.p, self.terms
-        for c, k in self.left[:count]:
-            j, T, s = p.off(DIMS[c][0], k), self.T[c], self.sem[c].at[k]
+        gate, up, down = self.terms
+        for part in self.left[:count]:
+            c, (i, j), s = part[0], self.at(part), self.sem.at[self.place[part]]
+            T = self.T[c].at[i, j]
             if c == "A":
                 for z in range(Z):
-                    src = (gate, up)[z // X].at[z // 2 % 2, j, :, :, z % 2, pl.ds(0, LEFT)]
-                    pltpu.make_async_copy(src, T.at[j, :, z], s).start()
+                    src = (gate, up)[z // X].at[z // 2 % 2, i, j, :, z % 2, pl.ds(0, LEFT)]
+                    pltpu.make_async_copy(src, T.at[z], s).start()
             elif c == "B":
-                for z in range(Z):
-                    layer, q = down_place(z)
-                    pltpu.make_async_copy(down.at[layer, :, j, q], T.at[j, z], s).start()
+                pltpu.make_async_copy(down.at[lax.rem(j, 2), :, i, lax.div(j, 2)], T, s).start()
             else:
-                layer, half = lax.rem(lax.div(j, 2), 2), lax.rem(j, 2)
+                layer, half = lax.rem(lax.div(i, 2), 2), lax.rem(i, 2)
 
                 def load(ref):
-                    pltpu.make_async_copy(ref.at[layer, :, :, :, half, pl.ds(LEFT, HALF - LEFT)], T.at[j], s).start()
-
-                pl.when(j < X)(lambda: load(gate))
-                pl.when(j >= X)(lambda: load(up))
+                    pltpu.make_async_copy(ref.at[layer, j, :, :, half, pl.ds(LEFT, HALF - LEFT)], T, s).start()
+
+                pl.when(i < X)(lambda: load(gate))
+                pl.when(i >= X)(lambda: load(up))
         self.left = self.left[count:]
 
-    def wait(self, c, k):
-        k %= lens(c)[0]
-        if (c, k) not in self.waited:
-            self.waited.add((c, k))
-            ref = self.T[c].at[self.p.off(DIMS[c][0], k)]
-            pltpu.make_async_copy(ref, ref, self.sem[c].at[k]).wait()
-            self.start(2)
+    def wait(self, part):
+        if part in self.place:
+            ref = self.T[part[0]].at[self.at(part)]
+            pltpu.make_async_copy(ref, ref, self.sem.at[self.place.pop(part)]).wait()
+            self.start(1)
 
 
 class Reduce:
@@ -275,7 +279,7 @@
         T, O = self.T[c], self.O[c]
         for w in REDUCE[t][2]:
             self.wait(w)
-        self.load.wait(c, d * k if phase == 1 else 0)
+        self.load.wait(block_of(t))
         src, first, _, _, count = self.areas(t)
         before = (c, phase, unit, d, k + 1)
         chain = before in R_ID
@@ -302,7 +306,7 @@
         for t in REDUCE:
             if t[0] == c and t[-1] == 1 and not any(t[2]):
                 self.wait(t)
-        self.load.wait(c, 0)
+        self.load.wait((c, 0, 0))
         i, j, k = (self.p.at[d] for d in DIMS[c])
         total = self.T[c][i, j, k].astype(F32)
         for part in self.ended(c, 3, j, k) + [(n1 - 1, n2 - 1, e) for e in (0, 1)]:
@@ -414,12 +418,12 @@
     outs, made, refs = refs[:3], refs[3:9], refs[9:]
     O, T, refs = dict(zip(COLOURS, outs)), dict(zip(COLOURS, refs)), refs[3:]
     s = dict(zip(SCRATCH, refs))
-    *load, small, turn, sent, arrived, few_sent, few_arrived = refs[len(SCRATCH) :]
+    load, small, turn, sent, arrived, few_sent, few_arrived = refs[len(SCRATCH) :]
     p = Place()
     x, y, z = p.at.values()
     all_here = greet(p)
-    loads = Loads(p, terms, T, dict(zip(COLOURS, load)))
-    loads.start(4)
+    loads = Loads(p, terms, T, load)
+    loads.start(AHEAD)
 
     def rows_fetch():
         first = (X * Y * PART) * x + 20 * y + lax.div(PART * z, 2)
@@ -574,7 +578,7 @@
         gather.send(t)
         if n > len(GATHER_ORDER) // 4 and n % 4 == 0 and later:
             later.pop(0)()
-    for t in ENDS:
+    for t in GATHER_ENDS:
         gather.wait(t)
     for wait in few.waits:
         wait()
@@ -649,7 +653,7 @@
             scratch_shapes=[
                 *shapes,
                 *(pltpu.VMEM(*a) for a in SCRATCH.values()),
-                *(semaphores(lens(c)[0]) for c in COLOURS),
+                semaphores(AHEAD),
                 semaphores(4),
                 pltpu.SemaphoreType.REGULAR,
                 *(semaphores(n) for n in (len(S_ID), len(R_ID), 6, 6)),

time: 230 us -> 227 us (0.987)
  Pallas kernels: 229 us -> 226 us
    pallas_call x1, Pallas kernels: 219 us -> 217 us  [step(): kernel(work, 'work', dict(collective_id=0, has_side_effects=True, vmem_li...]
where the time goes in v4:
time: 227 us
  Pallas kernels  226 us (100%)
    pallas_call x1, Pallas kernels, step(): kernel(work, 'work', dict(collective_id=0, has_side_effects=True, vmem_li...  217 us
    pallas_call x1, Pallas kernels, step(): kernel(put, 'put', dict(vmem_limit_bytes=1 << 20), out_shape=[jax.ShapeDt...  9.37 us

profile of v4, /device:TPU:2, one launch (start us, length us, event | category | flops | bytes accessed | tf_op | source)
XLA Modules:
  0.0 226.7 jit_solution(14734447139911800655)
XLA Ops:
  0.6 216.7 %work.1 = (bf16[4,4,8,7,6,8,128]{6,5,4,3,2,1,0:T(8,128)(2,1)S(1)}, bf16[4,8,4,5,7,8,128]{6,5,4,3,2,1,0:T(8,128)(2,1)S(1)}, bf16[8,4,4,7,4,8,128]{6,5,4,3,2,1,0:T...) custom-call(bf16[2,4,4,7,2,10,8,128]{7,6,5,4,3,2,1,0:T(8,128)(2,1)} , ...), custom_call_target="tpu_custom_call" | custom-call | tf_op jit(solution)/shard_map/work/pallas_call | solution.py:646
  217.3 9.4 %put.1 = (bf16[2,4,4,7,2,10,8,128]{7,6,5,4,3,2,1,0:T(8,128)(2,1)}, bf16[2,4,4,7,2,10,8,128]{7,6,5,4,3,2,1,0:T(8,128)(2,1)}, bf16[2,4,4,4,5,7,8,128]{7,6,5,4,3,2,...) custom-call(bf16[4,4,8,7,6,8,128]{6,5,4,3,2,1,0:T(8,128)(2,1)S(1)} %, ...), custom_call_target="tpu_custom_call" | custom-call | tf_op jit(solution)/shard_map/put/pallas_call | solution.py:662

commit v5 on v4

--- a/solution.py
+++ b/solution.py
@@ -58,7 +58,7 @@
     return (c, phase, unit, 1, n - o) if far else (c, phase, unit, -1, o)
 
 
-SECOND_BY_BLOCK, FIRST_BY_BLOCK = "AB", "A"
+SECOND_BY_BLOCK, FIRST_BY_BLOCK = "AC", "A"
 
 
 def gather_messages():
@@ -124,10 +124,10 @@
 
 
 GATHER = gather_messages()
-GATHER_ORDER, GATHER_ENDS = ordered(GATHER, 1.0, 2.0, 60.0)
-ENDS = ordered(GATHER, 0.5, 3.0, 50.0)[1]
-TURN = 67
-AHEAD = 12
+GATHER_ORDER, GATHER_ENDS = ordered(GATHER, 5.0, 2.0, 43.0)
+ENDS = ordered(GATHER, 4.0, 1.0, 50.0)[1]
+TURN = 59
+AHEAD = 8
 
 
 def back(t):
@@ -381,8 +381,8 @@
     "news": ((Z, HALF, *TILE), BF16),
     "new_low": ((LAYERS, 3, HIGH, *TILE), BF16),
     "news_low": ((2, 3, HIGH, *TILE), BF16),
-    "z_sum": ((Z, *TILE), F32),
-    "sum": ((X * Y, *TILE), F32),
+    "z_sum": ((Z, 1, LANES), F32),
+    "sum": ((X * Y, 1, LANES), F32),
 }
 
 
@@ -400,10 +400,26 @@
         self.waits.append(pltpu.make_async_copy(get, get, self.sent.at[i]).wait)
         return pltpu.make_async_copy(get, get, self.arrived.at[i]).wait
 
-    def line(self, out, into):
-        p = self.p
-        far = sorted(range(1, Z), key=lambda k: abs(k - X))
-        return self.exchange([(out.at[p.line[k]], into.at[p.at["z"]], p.line_device[k]) for k in far], into.at[pl.ds(0, Z - 1)])
+    def line(self, out, into, make):
+        p, i = self.p, len(self.waits)
+        z, get = p.at["z"], into.at[pl.ds(0, Z - 1)]
+        for k in range(Z):
+            make(k)
+
+            @pl.when(z != k)
+            def _():
+                pltpu.make_async_remote_copy(
+                    src_ref=out.at[k],
+                    dst_ref=into.at[z],
+                    send_sem=self.sent.at[i],
+                    recv_sem=self.arrived.at[i],
+                    device_id=p.device(z=k),
+                    device_id_type=MESH,
+                ).start()
+
+        into[z] = out[z]
+        self.waits.append(pltpu.make_async_copy(get, get, self.sent.at[i]).wait)
+        return pltpu.make_async_copy(get, get, self.arrived.at[i]).wait
 
     def tell(self, ref, at, devices):
         return self.exchange([(ref.at[at], ref.at[at], to) for to in devices], ref.at[pl.ds(0, len(devices))])
@@ -506,14 +522,14 @@
         else:
             s["own"][:, pl.ds(*((0, LEFT) if c == "A" else (LEFT, HALF - LEFT)))] = g
         squares = squares + jnp.sum((g * g).reshape(tiles(c), *TILE), axis=0)
-    s["z_sum"][z] = squares
+    s["z_sum"][z] = jnp.sum(squares, axis=0, keepdims=True)
     line_sums = few.tell(s["z_sum"], z, p.line_device[1:])
 
-    for k in range(Z):
+    def piece(k):
         at = s["own"][min(k, HIGH - 1)]
         s["out"][k] = (joined(s["own"][k - 1], at, k) if k else at).astype(BF16)
-    pieces = few.line(s["out"], s["into"])
-    s["into"][z] = s["out"][z]
+
+    pieces = few.line(s["out"], s["into"], piece)
     g = [s["own_low"][j] for j in range(PART)]
     for j in range(3):
         s["out_low"][0, j] = g[j].astype(BF16)
@@ -530,17 +546,17 @@
     pieces()
     pieces_low()
     sums()
-    total = jnp.sum(s["sum"][...], axis=0)
-    total = jnp.sum(jnp.sum(total, axis=1, keepdims=True), axis=0, keepdims=True)
+    total = jnp.sum(jnp.sum(s["sum"][...], axis=0), axis=1, keepdims=True)
     factor = jnp.minimum(1.0, 0.5 * lax.rsqrt(total / COUNT + 1e-30))
 
-    for owner in range(Z):
+    def step(owner):
         w, layer, part = owner // X, owner // 2 % 2, pl.ds(owner % 2 * HALF, HALF)
         g = s["into"][owner].astype(F32) * factor
         new, m, v = adamw(s["w"][w, layer, part], s["mv"][0, w, layer, part], s["mv"][1, w, layer, part], g)
         s["mv"][0, w, layer, part], s["mv"][1, w, layer, part] = m, v
         s["new"][owner] = new.astype(BF16)
-    pieces = few.line(s["new"], s["news"])
+
+    pieces = few.line(s["new"], s["news"], step)
     for layer in range(LAYERS):
         g = s["into_low"][layer].astype(F32) * factor
         new, m, v = adamw(s["w_low"][layer], s["mv_low"][0, layer], s["mv_low"][1, layer], g)
@@ -548,7 +564,6 @@
         s["new_low"][layer] = new.astype(BF16)
     pieces_low = few.exchange([(s["new_low"].at[other], s["news_low"].at[mine], partner)], s["news_low"].at[other])
     s["news_low"][mine] = s["new_low"][mine]
-    s["news"][z] = s["new"][z]
 
     own = {c: tuple(p.at[d] for d in DIMS[c]) for c in COLOURS}
 

time: 227 us -> 223 us (0.982)
  Pallas kernels: 226 us -> 223 us
    pallas_call x1, Pallas kernels: 217 us -> 213 us  [step(): kernel(work, 'work', dict(collective_id=0, has_side_effects=True, vmem_li...]
where the time goes in v5:
time: 223 us
  Pallas kernels  223 us (100%)
    pallas_call x1, Pallas kernels, step(): kernel(work, 'work', dict(collective_id=0, has_side_effects=True, vmem_li...  213 us
    pallas_call x1, Pallas kernels, step(): kernel(put, 'put', dict(vmem_limit_bytes=1 << 20), out_shape=[jax.ShapeDt...  9.37 us

profile of v5, /device:TPU:2, one launch (start us, length us, event | category | flops | bytes accessed | tf_op | source)
XLA Modules:
  0.0 223.2 jit_solution(2647081247620061521)
XLA Ops:
  0.6 213.1 %work.1 = (bf16[4,4,8,7,6,8,128]{6,5,4,3,2,1,0:T(8,128)(2,1)S(1)}, bf16[4,8,4,5,7,8,128]{6,5,4,3,2,1,0:T(8,128)(2,1)S(1)}, bf16[8,4,4,7,4,8,128]{6,5,4,3,2,1,0:T...) custom-call(bf16[2,4,4,7,2,10,8,128]{7,6,5,4,3,2,1,0:T(8,128)(2,1)} , ...), custom_call_target="tpu_custom_call" | custom-call | tf_op jit(solution)/shard_map/work/pallas_call | solution.py:661
  213.8 9.4 %put.1 = (bf16[2,4,4,7,2,10,8,128]{7,6,5,4,3,2,1,0:T(8,128)(2,1)}, bf16[2,4,4,7,2,10,8,128]{7,6,5,4,3,2,1,0:T(8,128)(2,1)}, bf16[2,4,4,4,5,7,8,128]{7,6,5,4,3,2,...) custom-call(bf16[4,4,8,7,6,8,128]{6,5,4,3,2,1,0:T(8,128)(2,1)S(1)} %, ...), custom_call_target="tpu_custom_call" | custom-call | tf_op jit(solution)/shard_map/put/pallas_call | solution.py:677

commit v6 on v5

--- a/solution.py
+++ b/solution.py
@@ -127,7 +127,7 @@
 GATHER_ORDER, GATHER_ENDS = ordered(GATHER, 5.0, 2.0, 43.0)
 ENDS = ordered(GATHER, 4.0, 1.0, 50.0)[1]
 TURN = 59
-AHEAD = 8
+AHEAD = 6
 
 
 def back(t):

time: 223 us -> 223 us (level)
  no operation moved by 1% of the time
where the time goes in v6:
time: 223 us
  Pallas kernels  222 us (100%)
    pallas_call x1, Pallas kernels, step(): kernel(work, 'work', dict(collective_id=0, has_side_effects=True, vmem_li...  213 us
    pallas_call x1, Pallas kernels, step(): kernel(put, 'put', dict(vmem_limit_bytes=1 << 20), out_shape=[jax.ShapeDt...  9.37 us

profile of v6, /device:TPU:2, one launch (start us, length us, event | category | flops | bytes accessed | tf_op | source)
XLA Modules:
  0.0 223.1 jit_solution(642554036382700782)
XLA Ops:
  0.6 213.1 %work.1 = (bf16[4,4,8,7,6,8,128]{6,5,4,3,2,1,0:T(8,128)(2,1)S(1)}, bf16[4,8,4,5,7,8,128]{6,5,4,3,2,1,0:T(8,128)(2,1)S(1)}, bf16[8,4,4,7,4,8,128]{6,5,4,3,2,1,0:T...) custom-call(bf16[2,4,4,7,2,10,8,128]{7,6,5,4,3,2,1,0:T(8,128)(2,1)} , ...), custom_call_target="tpu_custom_call" | custom-call | tf_op jit(solution)/shard_map/work/pallas_call | solution.py:661
  213.7 9.4 %put.1 = (bf16[2,4,4,7,2,10,8,128]{7,6,5,4,3,2,1,0:T(8,128)(2,1)}, bf16[2,4,4,7,2,10,8,128]{7,6,5,4,3,2,1,0:T(8,128)(2,1)}, bf16[2,4,4,4,5,7,8,128]{7,6,5,4,3,2,...) custom-call(bf16[4,4,8,7,6,8,128]{6,5,4,3,2,1,0:T(8,128)(2,1)S(1)} %, ...), custom_call_target="tpu_custom_call" | custom-call | tf_op jit(solution)/shard_map/put/pallas_call | solution.py:677
